TPU v7x, 32 devices: a whole 2x2x4 slice. The times are simulated.
32 devices in a mesh: gx: 4 (over y, core), gy: 4 (over z), gz: 2 (over x).
Axes of the slice: x: 2, y: 2, z: 4, core: 2. Of those that a mesh axis runs over, the one named last changes fastest.
Arguments:
- permittivity: float32 [32, 128, 256], P('gx', 'gy', 'gz'), may hold values from 1 to 9
- loss: float32 [32, 128, 256], P('gx', 'gy', 'gz'), may hold values from 0 to 0.2
- fwd_electric: float32 [3, 32, 128, 256], P(None, 'gx', 'gy', 'gz'), may hold values from -6 to 6
- fwd_magnetic: float32 [3, 32, 128, 256], P(None, 'gx', 'gy', 'gz'), may hold values from -6 to 6
- adj_electric: float32 [3, 32, 128, 256], P(None, 'gx', 'gy', 'gz'), may hold values from -200 to 200
- adj_magnetic: float32 [3, 32, 128, 256], P(None, 'gx', 'gy', 'gz'), may hold values from -200 to 200
- wavelet: float32 [64], replicated, may hold values from -6 to 6
- residuals: float32 [256, 64], P(('gx', 'gy', 'gz')), may hold values from -24 to 24
- source_cell: int32 [1], replicated, may hold values from 0 to 1048575
- receiver_cells: int32 [256], replicated, may hold values from 0 to 1048575
- start_step: int32 [1], replicated, may hold values from 0 to 60
Outputs:
- direction: float32 [32, 128, 256], P('gx', 'gy', 'gz')
- grad_rms: float32 [], replicated
Inputs may be any that keep to these rules, and one draw needn't show every extreme that they name: source_cell[0] is a flat index of a cell. receiver_cells[r] is the flat index of receiver r's cell; several receivers may share a cell. Samples start_step to start_step + 3 exist in every trace.
All inputs are finite; a program needn't handle non-finite values.
Results may differ from a plain program's by a relative error of at most 0.0003.
Values sent between devices are 32-bit elements; how exact they have to be, the bound alone decides.
A program may use at most 128 MiB of HBM per device.

v0:
```python
import functools

import jax
import jax.numpy as jnp
from jax import lax
from jax.experimental import pallas as pl
from jax.experimental.pallas import tpu as pltpu
from jax.sharding import PartitionSpec as P

STEPS = 4
MESH = pl.DeviceIdType.MESH
F32 = jnp.float32
HALF = 0.5


def kernel(
    sizes,
    wav_hbm,
    src_hbm,
    start_hbm,
    cells_hbm,
    perm_hbm,
    loss_hbm,
    fe_hbm,
    fm_hbm,
    ae_hbm,
    am_hbm,
    res_hbm,
    out_ref,
    rms_ref,
    E,
    H,
    perm,
    loss,
    keep,
    curl,
    D,
    A,
    inj,
    R,
    grad,
    ysend,
    yrecv,
    zsend,
    zrecv,
    part,
    sums,
    wav_ref,
    src_ref,
    start_ref,
    cells_ref,
    res_ref,
    mine,
    load_sem,
    face_send,
    face_recv,
    g_send,
    g_recv,
    r_send,
    r_recv,
):
    gx, gy, gz = sizes
    nx, ny, nz = perm.shape
    pad = E.shape[3] - ny
    ix, iy, iz = lax.axis_index("gx"), lax.axis_index("gy"), lax.axis_index("gz")
    nplane = gy * gz
    plane = iy * gz + iz

    loads = [
        pltpu.make_async_copy(fe_hbm, E.at[0, :, 0:nx, 0:ny, :], load_sem.at[0]),
        pltpu.make_async_copy(ae_hbm, E.at[1, :, 0:nx, 0:ny, :], load_sem.at[1]),
        pltpu.make_async_copy(fm_hbm, H.at[0, :, 1 : nx + 1, pad : pad + ny, :], load_sem.at[2]),
        pltpu.make_async_copy(am_hbm, H.at[1, :, 1 : nx + 1, pad : pad + ny, :], load_sem.at[3]),
        pltpu.make_async_copy(loss_hbm, loss, load_sem.at[4]),
        pltpu.make_async_copy(perm_hbm, perm, load_sem.at[5]),
    ]
    small = [
        pltpu.make_async_copy(start_hbm, start_ref, load_sem.at[6]),
        pltpu.make_async_copy(res_hbm, res_ref, load_sem.at[7]),
        pltpu.make_async_copy(src_hbm, src_ref, load_sem.at[8]),
        pltpu.make_async_copy(wav_hbm, wav_ref, load_sem.at[9]),
        pltpu.make_async_copy(cells_hbm, cells_ref, load_sem.at[10]),
    ]
    loads = loads + small
    for load in small:
        load.start()
    loads, small = loads[:6], loads[6:]
    for load in loads:
        load.start()

    total_devices = gx * nplane
    me = ix * nplane + plane
    peers = []
    for d in range(1, total_devices):
        q = lax.rem(me + d, total_devices)
        peers.append((q, (q // nplane, lax.rem(q // gz, gy), lax.rem(q, gz))))

    zero_plane = jnp.zeros((ny, nz), F32)
    for s in range(2):
        for c in range(3):
            E[s, c, nx, 0:ny, :] = zero_plane
            H[s, c, 0, pad : pad + ny, :] = zero_plane
    yrecv[...] = jnp.zeros(yrecv.shape, F32)
    zrecv[...] = jnp.zeros(zrecv.shape, F32)

    barrier = pltpu.get_barrier_semaphore()
    for _, dev in peers:
        pl.semaphore_signal(barrier, inc=1, device_id=dev, device_id_type=MESH)

    per, trace = res_hbm.shape
    small[0].wait()
    small[1].wait()
    begin = start_ref[0]
    time_at = lax.broadcasted_iota(jnp.int32, (trace, nz), 0)
    slot = lax.div(lax.broadcasted_iota(jnp.int32, (trace, nz), 1), per)
    pick = jnp.where(time_at == begin + STEPS - 1 - slot, 1.0, 0.0)
    wide = jnp.dot(res_ref[...], pick, precision=lax.Precision.HIGHEST, preferred_element_type=F32)
    own = lax.rem(lax.broadcasted_iota(jnp.int32, (per, nz), 1), per)
    own = own == lax.broadcasted_iota(jnp.int32, (per, nz), 0)
    mine[0] = jnp.sum(jnp.where(own, wide, 0.0), axis=0, keepdims=True)
    R[pl.ds(me, 1)] = mine[...]
    for load in small[2:]:
        load.wait()
    pl.semaphore_wait(barrier, len(peers))

    def remote(src, dst, ssem, rsem, dev):
        return pltpu.make_async_remote_copy(
            src_ref=src, dst_ref=dst, send_sem=ssem, recv_sem=rsem,
            device_id=dev, device_id_type=MESH,
        )

    def exchange(src, slots, send_sems, recv_sems):
        copies = []
        for d, (q, dev) in enumerate(peers):
            send = remote(src, slots.at[me], send_sems.at[d], recv_sems.at[me], dev)
            recv = remote(src, slots.at[q], send_sems.at[d], recv_sems.at[q], dev)
            send.start()
            copies.append((send, recv))
        return copies

    def settle(copies):
        for send, recv in copies:
            recv.wait_recv()
        for send, recv in copies:
            send.wait_send()

    def faces(s, kind):
        low = kind == 0
        step = -1 if low else 1
        field = E if low else H
        rows = slice(0, ny) if low else slice(pad, pad + ny)
        from_x, to_x = (0, nx) if low else (nx, 0)
        idx = (ix, iy, iz)
        size = (gx, gy, gz)
        refs = (
            (field.at[s, 1:3, from_x, rows, :], field.at[s, 1:3, to_x, rows, :]),
            (ysend.at[kind, s], yrecv.at[kind, s]),
            (zsend.at[kind, s], zrecv.at[kind, s]),
        )
        out = []
        for a in range(3):
            if low:
                can_send, can_recv = idx[a] > 0, idx[a] < size[a] - 1
            else:
                can_send, can_recv = idx[a] < size[a] - 1, idx[a] > 0
            dev = [ix, iy, iz]
            dev[a] = jnp.clip(idx[a] + step, 0, size[a] - 1)
            copy = remote(refs[a][0], refs[a][1], face_send.at[kind, s, a], face_recv.at[kind, s, a], tuple(dev))
            out.append((copy, can_send, can_recv))
        return out

    def start(face, extra=None):
        copy, can_send, _ = face
        cond = can_send if extra is None else can_send & extra

        @pl.when(cond)
        def _():
            copy.start()

    def finish(face):
        copy, can_send, _ = face

        @pl.when(can_send)
        def _():
            copy.wait_send()

    def arrive(face):
        copy, _, can_recv = face

        @pl.when(can_recv)
        def _():
            copy.wait_recv()

    lane = lax.broadcasted_iota(jnp.int32, (ny, nz), 1)
    row = lax.broadcasted_iota(jnp.int32, (ny, nz), 0)

    def pack_column(acc, value, source, j):
        return jnp.where(lane == j, pltpu.roll(value, (j - source) % nz, 1), acc)

    def up_z(value, halo, j):
        return jnp.where(lane == nz - 1, pltpu.roll(halo, (nz - 1 - j) % nz, 1), pltpu.roll(value, nz - 1, 1))

    def down_z(value, halo, j):
        rolled = pltpu.roll(value, 1, 1)
        return jnp.where(lane == 0, pltpu.roll(halo, (nz - j) % nz, 1), rolled)

    def send_first(s):
        acc = jnp.zeros((ny, nz), F32)
        face = faces(s, 0)
        start(face[0])
        for p in range(nx):
            ysend[0, s, 0, p : p + 1, :] = E[s, 0, p, 0:1, :]
            ysend[0, s, 1, p : p + 1, :] = E[s, 2, p, 0:1, :]
            acc = pack_column(acc, E[s, 0, p, 0:ny, :], 0, p)
            acc = pack_column(acc, E[s, 1, p, 0:ny, :], 0, nx + p)
        zsend[0, s] = acc
        start(face[1])
        start(face[2])

    def update_h(s):
        came = faces(s, 0)
        going = faces(s, 1)
        for face in came:
            arrive(face)
        for p in range(nx):
            E[s, 0, p, ny : ny + 1, :] = yrecv[0, s, 0, p : p + 1, :]
            E[s, 2, p, ny : ny + 1, :] = yrecv[0, s, 1, p : p + 1, :]
        halo = zrecv[0, s]
        acc = jnp.zeros((ny, nz), F32)
        inner = slice(pad, pad + ny)
        for p in reversed(range(nx)):
            ex, ey, ez = E[s, 0, p, 0:ny, :], E[s, 1, p, 0:ny, :], E[s, 2, p, 0:ny, :]
            hx = H[s, 0, p + 1, inner, :] - HALF * (E[s, 2, p, 1 : ny + 1, :] - ez - (up_z(ey, halo, nx + p) - ey))
            hy = H[s, 1, p + 1, inner, :] - HALF * (up_z(ex, halo, p) - ex - (E[s, 2, p + 1, 0:ny, :] - ez))
            hz = H[s, 2, p + 1, inner, :] - HALF * (E[s, 1, p + 1, 0:ny, :] - ey - (E[s, 0, p, 1 : ny + 1, :] - ex))
            H[s, 0, p + 1, inner, :] = hx
            H[s, 1, p + 1, inner, :] = hy
            H[s, 2, p + 1, inner, :] = hz
            if p == nx - 1:
                start(going[0])
            ysend[1, s, 0, p : p + 1, :] = hx[ny - 1 : ny, :]
            ysend[1, s, 1, p : p + 1, :] = hz[ny - 1 : ny, :]
            acc = pack_column(acc, hx, nz - 1, p)
            acc = pack_column(acc, hy, nz - 1, nx + p)
        zsend[1, s] = acc
        start(going[1])
        start(going[2])

    src = src_ref[0]
    total_z, total_y = nz * gz, ny * gy
    src_i = lax.div(src, total_y * total_z) - ix * nx
    src_j = lax.rem(lax.div(src, total_z), total_y) - iy * ny
    src_k = lax.rem(src, total_z) - iz * nz
    src_mask = (row == src_j) & (lane == src_k)

    def update_e(s, k):
        came = faces(s, 1)
        going = faces(s, 0)
        for face in came:
            arrive(face)
        for face in going:
            finish(face)
        for p in range(nx):
            H[s, 0, p + 1, pad - 1 : pad, :] = yrecv[1, s, 0, p : p + 1, :]
            H[s, 2, p + 1, pad - 1 : pad, :] = yrecv[1, s, 1, p : p + 1, :]
        more = k < STEPS - 1
        halo = zrecv[1, s]
        acc = jnp.zeros((ny, nz), F32)
        inner = slice(pad, pad + ny)
        below = slice(pad - 1, pad + ny - 1)
        pulse = wav_ref[begin + k]
        for p in range(nx):
            hx, hy, hz = H[s, 0, p + 1, inner, :], H[s, 1, p + 1, inner, :], H[s, 2, p + 1, inner, :]
            kp, cl = keep[p], curl[p]
            ox, oy, oz = E[s, 0, p, 0:ny, :], E[s, 1, p, 0:ny, :], E[s, 2, p, 0:ny, :]
            ex = kp * ox + cl * (hz - H[s, 2, p + 1, below, :] - (hy - down_z(hy, halo, nx + p)))
            ey = kp * oy + cl * (hx - down_z(hx, halo, p) - (hz - H[s, 2, p, inner, :]))
            ez = kp * oz + cl * (hy - H[s, 1, p, inner, :] - (hx - H[s, 0, p + 1, below, :]))
            if s == 0:
                ez = ez + jnp.where(src_mask, jnp.where(src_i == p, pulse, 0.0), 0.0)
                D[k, 0, p] = ex - ox
                D[k, 1, p] = ey - oy
                D[k, 2, p] = ez - oz
            else:
                ez = ez + inj[k, p * ny : (p + 1) * ny, :]
                A[k, 0, p] = ex
                A[k, 1, p] = ey
                A[k, 2, p] = ez
            E[s, 0, p, 0:ny, :] = ex
            E[s, 1, p, 0:ny, :] = ey
            E[s, 2, p, 0:ny, :] = ez
            if p == 0:
                start(going[0], more)
            ysend[0, s, 0, p : p + 1, :] = ex[0:1, :]
            ysend[0, s, 1, p : p + 1, :] = ez[0:1, :]
            acc = pack_column(acc, ex, 0, p)
            acc = pack_column(acc, ey, 0, nx + p)
        zsend[0, s] = acc
        start(going[1], more)
        start(going[2], more)
        for face in came_out(s):
            finish(face)

    def came_out(s):
        return faces(s, 1)

    def injection():
        cells = cells_ref[...]
        count = cells.shape[1]
        i = lax.div(cells, total_y * total_z) - ix * nx
        j = lax.rem(lax.div(cells, total_z), total_y) - iy * ny
        k = lax.rem(cells, total_z) - iz * nz
        inside = (i >= 0) & (i < nx) & (j >= 0) & (j < ny)
        where = jnp.where(inside, i * ny + j, -1)
        rows = lax.broadcasted_iota(jnp.int32, (nx * ny, count), 0)
        spots = jnp.where(rows == where, 1.0, 0.0).astype(jnp.bfloat16)
        depth = lax.broadcasted_iota(jnp.int32, (nz, count), 0) == k
        nt = (((1,), (1,)), ((), ()))
        spread_lane = lax.broadcasted_iota(jnp.int32, (nz, count), 0)
        spread_rec = lax.rem(lax.broadcasted_iota(jnp.int32, (nz, count), 1), per)
        holder = lax.div(lax.broadcasted_iota(jnp.int32, (total_devices, count), 1), per)
        holder = holder == lax.broadcasted_iota(jnp.int32, (total_devices, count), 0)
        packed = R[:, 0, :]
        for m in range(STEPS):
            spread = jnp.where(spread_lane == m * per + spread_rec, 1.0, 0.0)
            found = jnp.dot(packed, spread, precision=lax.Precision.HIGHEST, preferred_element_type=F32)
            samples = jnp.sum(jnp.where(holder, found, 0.0), axis=0, keepdims=True)
            rest = jnp.where(depth, samples, 0.0)
            total = jnp.zeros((nx * ny, nz), F32)
            for _ in range(3):
                head = rest.astype(jnp.bfloat16)
                rest = rest - head.astype(F32)
                total = total + lax.dot_general(spots, head, nt, preferred_element_type=F32)
            inj[m] = total

    loads[0].wait()
    send_first(0)
    loads[1].wait()
    send_first(1)
    gather = exchange(mine.at[0], R, g_send, g_recv)
    loads[4].wait()
    loads[5].wait()
    for p in range(nx):
        lo = loss[p]
        keep[p] = (1.0 - lo) / (1.0 + lo)
        curl[p] = 0.5 / (perm[p] * (1.0 + lo))
    loads[2].wait()
    loads[3].wait()

    update_h(0)
    update_h(1)
    update_e(0, 0)
    settle(gather)
    injection()
    update_e(1, 0)

    def body(k, carry):
        update_h(0)
        update_h(1)
        update_e(0, k)
        update_e(1, k)
        return carry

    lax.fori_loop(1, STEPS, body, 0)

    squares = jnp.zeros((ny, nz), F32)
    for p in range(nx):
        total = jnp.zeros((ny, nz), F32)
        for m in range(STEPS):
            n = STEPS - 1 - m
            total = total + (D[n, 0, p] * A[m, 0, p] + D[n, 1, p] * A[m, 1, p] + D[n, 2, p] * A[m, 2, p])
        g = -total / perm[p]
        grad[p] = g
        squares = squares + g * g
    part[0] = jnp.sum(squares, axis=0, keepdims=True)
    sums[pl.ds(me, 1)] = part[...]
    settle(exchange(part.at[0], sums, r_send, r_recv))
    tile = sums[:, 0, :]
    total = jnp.sum(jnp.sum(tile, axis=0, keepdims=True), axis=1, keepdims=True)
    rms = jnp.sqrt(total / (nx * ny * nz * gx * gy * gz) + 1e-06)
    rms_ref[...] = rms
    inverse = 1.0 / rms
    for p in range(nx):
        out_ref[p] = grad[p] * inverse


def per_device(
    permittivity, loss, fwd_electric, fwd_magnetic, adj_electric, adj_magnetic,
    wavelet, residuals, source_cell, receiver_cells, start_step,
):
    sizes = tuple(lax.axis_size(a) for a in ("gx", "gy", "gz"))
    gx, gy, gz = sizes
    nx, ny, nz = permittivity.shape
    devices = gx * gy * gz
    count = receiver_cells.shape[0]
    vmem = pl.BlockSpec(memory_space=pltpu.VMEM)
    hbm = pl.BlockSpec(memory_space=pltpu.HBM)
    dma = pltpu.SemaphoreType.DMA
    block = (nx, ny, nz)
    padded = (2, 3, nx + 1, ny + 8, nz)
    direction, rms = pl.pallas_call(
        functools.partial(kernel, sizes),
        out_shape=(
            pltpu.VMEM(block, F32),
            jax.ShapeDtypeStruct((1, 1), F32),
        ),
        in_specs=[hbm] * 11,
        out_specs=(vmem, vmem),
        scratch_shapes=[
            pltpu.VMEM(padded, F32),
            pltpu.VMEM(padded, F32),
            pltpu.VMEM(block, F32),
            pltpu.VMEM(block, F32),
            pltpu.VMEM(block, F32),
            pltpu.VMEM(block, F32),
            pltpu.VMEM((STEPS, 3) + block, F32),
            pltpu.VMEM((STEPS, 3) + block, F32),
            pltpu.VMEM((STEPS, nx * ny, nz), F32),
            pltpu.VMEM((devices, 1, nz), F32),
            pltpu.VMEM(block, F32),
            pltpu.VMEM((2, 2, 2, nx, nz), F32),
            pltpu.VMEM((2, 2, 2, nx, nz), F32),
            pltpu.VMEM((2, 2, ny, nz), F32),
            pltpu.VMEM((2, 2, ny, nz), F32),
            pltpu.VMEM((1, 1, nz), F32),
            pltpu.VMEM((devices, 1, nz), F32),
            pltpu.SMEM(wavelet.shape, F32),
            pltpu.SMEM((1,), jnp.int32),
            pltpu.SMEM((1,), jnp.int32),
            pltpu.VMEM((1, count), jnp.int32),
            pltpu.VMEM(residuals.shape, F32),
            pltpu.VMEM((1, 1, nz), F32),
            dma((11,)),
            dma((2, 2, 3)),
            dma((2, 2, 3)),
            dma((devices,)),
            dma((devices,)),
            dma((devices,)),
            dma((devices,)),
        ],
        compiler_params=pltpu.CompilerParams(
            collective_id=0, has_side_effects=True, vmem_limit_bytes=60 * 1024 * 1024
        ),
    )(
        wavelet, source_cell, start_step, receiver_cells.reshape(1, count),
        permittivity, loss, fwd_electric, fwd_magnetic, adj_electric, adj_magnetic, residuals,
    )
    return direction, rms.reshape(())


def solution(mesh):
    block = P("gx", "gy", "gz")
    state = P(None, "gx", "gy", "gz")
    return jax.shard_map(
        per_device,
        mesh=mesh,
        in_specs=(
            block, block, state, state, state, state,
            P(), P(("gx", "gy", "gz"), None), P(), P(), P(),
        ),
        out_specs=(block, P()),
        check_vma=False,
    )
```

profile of v0, /device:TPU:0, one launch (start us, length us, event | category | flops | bytes accessed | tf_op | source)
XLA Modules:
  0.0 44.4 jit_solution(3022605681039413249)
XLA Ops:
  1.9 40.1 %shard_map.122 = (f32[8,32,128]{2,1,0:T(8,128)S(1)}, f32[1,1]{1,0:T(1,128)}) custom-call(f32[64]{0:T(128)} %wav_hbm.1, s32[1]{0:T(128)S(6)} %copy.16.src_hbm, s32[1]{0:T(128)S(6)} %copy.17.start_hbm, s32[1,256]{1,0:T(1,128)} %bitcast.2, f32[8,32,128]{2,1,0:T(8,128)} %perm_hbm.1, f32[8,32,128]{2,1,0:T(8,128)} %loss_hbm.1, f32[3,8,32,128]{3,2,1,0:T(8,128)} %fe_hbm.1, ...), custom_call_target="tpu_custom_call" | custom-call | tf_op jit(solution)/shard_map/pallas_call | solution.py:401
  42.0 0.7 %copy.15 = f32[8,32,128]{2,1,0:T(8,128)} copy(f32[8,32,128]{2,1,0:T(8,128)S(1)} %get-tuple-element.6) | data formatting | bytes 262144
where the time goes:
time: 44.5 us; the launch traced here: 44.4 us
  Pallas kernels  40.1 us (90%)
  between operations  3.62 us (8%)
  local copies, waits for them, and re-layouts  0.66 us (1%)
    pallas_call x1, Pallas kernels, per_device(): pl.pallas_call(functools.partial(kernel, sizes), out_shape=(pltpu.VMEM(bl...  40.1 us

commit v1 on v0

v1 whole, which is shorter than its diff:
```python
import functools

import jax
import jax.numpy as jnp
from jax import lax
from jax.experimental import pallas as pl
from jax.experimental.pallas import tpu as pltpu
from jax.sharding import PartitionSpec as P

STEPS = 4
MESH = pl.DeviceIdType.MESH
F32 = jnp.float32
HALF = 0.5


def kernel(
    sizes,
    wav_hbm,
    src_hbm,
    start_hbm,
    cells_hbm,
    perm_hbm,
    loss_hbm,
    fe_hbm,
    fm_hbm,
    ae_hbm,
    am_hbm,
    res_hbm,
    out_ref,
    rms_ref,
    E,
    H,
    perm,
    loss,
    keep,
    curl,
    D,
    A,
    inj,
    R_all,
    grad,
    HP,
    xU,
    xD,
    ysU,
    ysD,
    yU,
    yD,
    zsU,
    zsD,
    zU,
    zD,
    zX,
    zXU,
    e1s,
    e2s,
    e1r,
    e2r,
    hys,
    hyr,
    hzs,
    part,
    sums,
    wav_ref,
    src_ref,
    start_ref,
    cells_ref,
    res_ref,
    mine,
    load_sem,
    f_send,
    f_recv,
    h_send,
    h_recv,
    g_send,
    g_recv,
    r_send,
    r_recv,
):
    gx, gy, gz = sizes
    nx, ny, nz = perm.shape
    pad = H.shape[3] - ny
    O = slice(pad, pad + ny)
    R = slice(0, pad + ny)
    above = slice(pad + 1, pad + ny + 1)
    ix, iy, iz = lax.axis_index("gx"), lax.axis_index("gy"), lax.axis_index("gz")
    nplane = gy * gz
    plane = iy * gz + iz

    loads = [
        pltpu.make_async_copy(fe_hbm, E.at[0, :, :, O, :], load_sem.at[0]),
        pltpu.make_async_copy(ae_hbm, E.at[1, :, :, O, :], load_sem.at[1]),
        pltpu.make_async_copy(fm_hbm, H.at[0, :, 1 : nx + 1, O, :], load_sem.at[2]),
        pltpu.make_async_copy(am_hbm, H.at[1, :, 1 : nx + 1, O, :], load_sem.at[3]),
        pltpu.make_async_copy(loss_hbm, loss, load_sem.at[4]),
        pltpu.make_async_copy(perm_hbm, perm, load_sem.at[5]),
    ]
    small = [
        pltpu.make_async_copy(start_hbm, start_ref, load_sem.at[6]),
        pltpu.make_async_copy(res_hbm, res_ref, load_sem.at[7]),
        pltpu.make_async_copy(src_hbm, src_ref, load_sem.at[8]),
        pltpu.make_async_copy(wav_hbm, wav_ref, load_sem.at[9]),
        pltpu.make_async_copy(cells_hbm, cells_ref, load_sem.at[10]),
    ]
    loads = loads + small
    for load in small:
        load.start()
    loads, small = loads[:6], loads[6:]
    for load in loads:
        load.start()

    total_devices = gx * nplane
    me = ix * nplane + plane
    peers = []
    for d in range(1, total_devices):
        q = lax.rem(me + d, total_devices)
        peers.append((q, (q // nplane, lax.rem(q // gz, gy), lax.rem(q, gz))))

    zero_plane = jnp.zeros((ny, nz), F32)
    zero_tile = jnp.zeros((pad, nz), F32)
    for s in range(2):
        for c in range(3):
            H[s, c, 0, O, :] = zero_plane
            for p in range(nx):
                E[s, c, p, 0:pad, :] = zero_tile
                E[s, c, p, pad + ny : pad + ny + pad, :] = zero_tile
                H[s, c, p + 1, 0:pad, :] = zero_tile
    for buffer in (HP, xU, xD, yU, yD, zU, zD, zX, zXU, e1r, e2r, hyr):
        buffer[...] = jnp.zeros(buffer.shape, F32)

    barrier = pltpu.get_barrier_semaphore()
    for _, dev in peers:
        pl.semaphore_signal(barrier, inc=1, device_id=dev, device_id_type=MESH)

    per, trace = res_hbm.shape
    small[0].wait()
    small[1].wait()
    begin = start_ref[0]
    time_at = lax.broadcasted_iota(jnp.int32, (trace, nz), 0)
    slot = lax.div(lax.broadcasted_iota(jnp.int32, (trace, nz), 1), per)
    pick = jnp.where(time_at == begin + STEPS - 1 - slot, 1.0, 0.0)
    wide = jnp.dot(res_ref[...], pick, precision=lax.Precision.HIGHEST, preferred_element_type=F32)
    own = lax.rem(lax.broadcasted_iota(jnp.int32, (per, nz), 1), per)
    own = own == lax.broadcasted_iota(jnp.int32, (per, nz), 0)
    mine[0] = jnp.sum(jnp.where(own, wide, 0.0), axis=0, keepdims=True)
    R_all[pl.ds(me, 1)] = mine[...]
    for load in small[2:]:
        load.wait()
    pl.semaphore_wait(barrier, len(peers))

    def remote(src, dst, ssem, rsem, dev):
        return pltpu.make_async_remote_copy(
            src_ref=src, dst_ref=dst, send_sem=ssem, recv_sem=rsem,
            device_id=dev, device_id_type=MESH,
        )

    def exchange(src, slots, send_sems, recv_sems):
        copies = []
        for d, (q, dev) in enumerate(peers):
            send = remote(src, slots.at[me], send_sems.at[d], recv_sems.at[me], dev)
            recv = remote(src, slots.at[q], send_sems.at[d], recv_sems.at[q], dev)
            send.start()
            copies.append((send, recv))
        return copies

    def settle(copies):
        for send, recv in copies:
            recv.wait_recv()
        for send, recv in copies:
            send.wait_send()

    has = {
        "+x": ix < gx - 1, "-x": ix > 0, "+y": iy < gy - 1,
        "-y": iy > 0, "+z": iz < gz - 1, "-z": iz > 0,
    }
    flip = {"+": "-", "-": "+"}

    def route(steps):
        dev = [ix, iy, iz]
        size = (gx, gy, gz)
        can_send, can_recv = True, True
        for step in steps:
            axis = "xyz".index(step[1])
            dev[axis] = jnp.clip(dev[axis] + (1 if step[0] == "+" else -1), 0, size[axis] - 1)
            back = flip[step[0]] + step[1]
            can_send = has[step] if can_send is True else can_send & has[step]
            can_recv = has[back] if can_recv is True else can_recv & has[back]
        return tuple(dev), can_send, can_recv

    def face(s, slot, d):
        table = (
            (("+x",), E.at[s, :, nx - 1, O, :], xU.at[slot, s, :, O, :]),
            (("-x",), E.at[s, 1:3, 0, O, :], xD.at[slot, s, :, O, :]),
            (("+y",), ysU.at[s], yU.at[slot, s]),
            (("-y",), ysD.at[s], yD.at[slot, s]),
            (("+z",), zsU.at[s], zU.at[slot, s, 0:ny, :]),
            (("-z",), zsD.at[s], zD.at[slot, s, O, :]),
            (("+x", "-y"), e1s.at[s], e1r.at[slot, s]),
            (("-x", "+y"), e2s.at[s], e2r.at[slot, s]),
            (("+x", "-z"), zsD.at[s], zX.at[slot, s]),
            (("-x", "+z"), zsU.at[s], zXU.at[slot, s]),
            (("+y", "-z"), zsD.at[s, ny - pad : ny, :], zD.at[slot, s, 0:pad, :]),
            (("-y", "+z"), zsU.at[s, 0:pad, :], zU.at[slot, s, ny : ny + pad, :]),
        )
        steps, source, target = table[d]
        dev, can_send, can_recv = route(steps)
        return remote(source, target, f_send.at[s, d], f_recv.at[slot, s, d], dev), can_send, can_recv

    def first(s, d):
        table = (
            (("+x",), H.at[s, 1:3, nx, O, :], H.at[s, 1:3, 0, O, :]),
            (("+y",), hys.at[s], hyr.at[s]),
            (("+z",), hzs.at[s], HP.at[s]),
        )
        steps, source, target = table[d]
        dev, can_send, can_recv = route(steps)
        return remote(source, target, h_send.at[s, d], h_recv.at[s, d], dev), can_send, can_recv

    def start(item):
        copy, can_send, _ = item

        @pl.when(can_send)
        def _():
            copy.start()

    def finish(item):
        copy, can_send, _ = item

        @pl.when(can_send)
        def _():
            copy.wait_send()

    def arrive(item):
        copy, _, can_recv = item

        @pl.when(can_recv)
        def _():
            copy.wait_recv()

    lane = lax.broadcasted_iota(jnp.int32, (ny, nz), 1)
    row = lax.broadcasted_iota(jnp.int32, (ny, nz), 0)

    def pack_column(acc, value, source, j):
        return jnp.where(lane == j, pltpu.roll(value, (j - source) % nz, 1), acc)

    def down_z(value, halo, j):
        rolled = pltpu.roll(value, 1, 1)
        return jnp.where(lane == 0, pltpu.roll(halo, (nz - j) % nz, 1), rolled)

    def pack_rows(s):
        for p in range(nx):
            for c in range(3):
                ysU[s, c, p : p + 1, :] = E[s, c, p, pad + ny - 1 : pad + ny, :]
            ysD[s, 0, p : p + 1, :] = E[s, 0, p, pad : pad + 1, :]
            ysD[s, 1, p : p + 1, :] = E[s, 2, p, pad : pad + 1, :]
        e1s[s] = E[s, 0, nx - 1, pad : pad + 1, :]
        e2s[s] = E[s, 1, 0, pad + ny - 1 : pad + ny, :]

    def pack_low(s):
        @pl.when(has["-z"])
        def _():
            acc = jnp.zeros((ny, nz), F32)
            for p in range(nx):
                acc = pack_column(acc, E[s, 0, p, O, :], 0, p)
                acc = pack_column(acc, E[s, 1, p, O, :], 0, nx + p)
            zsD[s] = acc

    def pack_high(s):
        @pl.when(has["+z"])
        def _():
            acc = jnp.zeros((ny, nz), F32)
            for p in range(nx):
                acc = pack_column(acc, E[s, 0, p, O, :], nz - 1, p)
                acc = pack_column(acc, E[s, 1, p, O, :], nz - 1, nx + p)
                acc = pack_column(acc, E[s, 2, p, O, :], nz - 1, 2 * nx + p)
            zsU[s] = acc

    def send_rest(s, slot):
        pack_rows(s)
        for d in (6, 7, 2, 3):
            start(face(s, slot, d))
        pack_low(s)
        pack_high(s)
        for d in (8, 9, 10, 11, 4, 5):
            start(face(s, slot, d))

    def send_magnetic(s):
        start(first(s, 0))
        for p in range(nx):
            hys[s, 0, p : p + 1, :] = H[s, 0, p + 1, pad + ny - 1 : pad + ny, :]
            hys[s, 1, p : p + 1, :] = H[s, 2, p + 1, pad + ny - 1 : pad + ny, :]
        start(first(s, 1))

        @pl.when(has["+z"])
        def _():
            acc = jnp.zeros((ny, nz), F32)
            for p in range(nx):
                acc = pack_column(acc, H[s, 1, p + 1, O, :], nz - 1, p)
                acc = pack_column(acc, H[s, 0, p + 1, O, :], nz - 1, nx + p)
            hzs[s] = acc

        start(first(s, 2))

    half_x = jnp.where(has["-x"], HALF, 0.0)
    half_rows = jnp.where(lax.broadcasted_iota(jnp.int32, (pad + ny, nz), 0) < pad, jnp.where(has["-y"], HALF, 0.0), HALF)
    lane_r = lax.broadcasted_iota(jnp.int32, (pad + ny, nz), 1)

    def up_z(value, halo, j):
        edge = lane_r[: value.shape[0]] == nz - 1
        return jnp.where(edge, pltpu.roll(halo, (nz - 1 - j) % nz, 1), pltpu.roll(value, nz - 1, 1))

    def update_h(s, slot, opening):
        for d in (2, 3, 5, 10):
            arrive(face(s, slot, d))
        if opening:
            arrive(first(s, 1))
            for p in range(nx):
                H[s, 0, p + 1, pad - 1 : pad, :] = hyr[s, 0, p : p + 1, :]
                H[s, 2, p + 1, pad - 1 : pad, :] = hyr[s, 1, p : p + 1, :]
        for p in range(nx):
            for c in range(3):
                E[s, c, p, pad - 1 : pad, :] = yU[slot, s, c, p : p + 1, :]
            E[s, 0, p, pad + ny : pad + ny + 1, :] = yD[slot, s, 0, p : p + 1, :]
            E[s, 2, p, pad + ny : pad + ny + 1, :] = yD[slot, s, 1, p : p + 1, :]
        halo = zD[slot, s]
        up = slice(1, pad + ny + 1)
        for p in range(nx):
            if p == nx - 1:
                for d in (0, 1, 6, 7, 8):
                    arrive(face(s, slot, d))
                xU[slot, s, 0, pad + ny : pad + ny + 1, :] = e1r[slot, s]
                xD[slot, s, 0, pad - 1 : pad, :] = e2r[slot, s]
                next_y, next_z = xD[slot, s, 0, R, :], xD[slot, s, 1, O, :]
            else:
                next_y, next_z = E[s, 1, p + 1, R, :], E[s, 2, p + 1, O, :]
            ex, ey, ez = E[s, 0, p, R, :], E[s, 1, p, R, :], E[s, 2, p, R, :]
            hx = H[s, 0, p + 1, R, :] - half_rows * (E[s, 2, p, up, :] - ez - (up_z(ey, halo, nx + p) - ey))
            hy = H[s, 1, p + 1, O, :] - HALF * (up_z(ex[pad:], halo[pad:], p) - ex[pad:] - (next_z - ez[pad:]))
            hz = H[s, 2, p + 1, R, :] - half_rows * (next_y - ey - (E[s, 0, p, up, :] - ex))
            H[s, 0, p + 1, R, :] = hx
            H[s, 1, p + 1, O, :] = hy
            H[s, 2, p + 1, R, :] = hz
        if opening:
            arrive(first(s, 0))
        ex, ey, ez = xU[slot, s, 0, O, :], xU[slot, s, 1, O, :], xU[slot, s, 2, O, :]
        side = H[s, 1, 0, O, :] - half_x * (up_z(ex, zX[slot, s], nx - 1) - ex - (E[s, 2, 0, O, :] - ez))
        H[s, 1, 0, O, :] = side
        side = H[s, 2, 0, O, :] - half_x * (E[s, 1, 0, O, :] - ey - (xU[slot, s, 0, above, :] - ex))
        H[s, 2, 0, O, :] = side
        for d in (4, 9, 11):
            arrive(face(s, slot, d))
        if opening:
            arrive(first(s, 2))

        @pl.when(has["-z"])
        def _():
            below = zU[slot, s, 0:ny, :]
            wide = jnp.where(lane == 3 * nx, pltpu.roll(zXU[slot, s], nx, 1), below)
            along = pltpu.roll(pltpu.roll(wide, nz - 1, 1) - wide, nz - 2 * nx, 1)
            across = pltpu.roll(zU[slot, s, 1 : ny + 1, :] - below, nz - nx, 1)
            turn = jnp.where(lane < nx, along, across)
            HP[s] = HP[s] - jnp.where(lane < nx, HALF, -HALF) * (zsD[s] - below - turn)

    src = src_ref[0]
    total_z, total_y = nz * gz, ny * gy
    src_i = lax.div(src, total_y * total_z) - ix * nx
    src_j = lax.rem(lax.div(src, total_z), total_y) - iy * ny
    src_k = lax.rem(src, total_z) - iz * nz
    src_mask = (row == src_j) & (lane == src_k)

    def update_e(s, k, slot):
        for d in range(12):
            finish(face(s, slot, d))
        more = k < STEPS - 1
        halo = HP[s]
        below = slice(pad - 1, pad + ny - 1)
        pulse = wav_ref[begin + k]
        for p in (nx - 1,) + tuple(range(nx - 1)):
            hx, hy, hz = H[s, 0, p + 1, O, :], H[s, 1, p + 1, O, :], H[s, 2, p + 1, O, :]
            kp, cl = keep[p], curl[p]
            ox, oy, oz = E[s, 0, p, O, :], E[s, 1, p, O, :], E[s, 2, p, O, :]
            ex = kp * ox + cl * (hz - H[s, 2, p + 1, below, :] - (hy - down_z(hy, halo, p)))
            ey = kp * oy + cl * (hx - down_z(hx, halo, nx + p) - (hz - H[s, 2, p, O, :]))
            ez = kp * oz + cl * (hy - H[s, 1, p, O, :] - (hx - H[s, 0, p + 1, below, :]))
            if s == 0:
                ez = ez + jnp.where(src_mask, jnp.where(src_i == p, pulse, 0.0), 0.0)
                D[k, 0, p] = ex - ox
                D[k, 1, p] = ey - oy
                D[k, 2, p] = ez - oz
            else:
                ez = ez + inj[k, p * ny : (p + 1) * ny, :]
                A[k, 0, p] = ex
                A[k, 1, p] = ey
                A[k, 2, p] = ez
            E[s, 0, p, O, :] = ex
            E[s, 1, p, O, :] = ey
            E[s, 2, p, O, :] = ez
            if p == nx - 1 or p == 0:
                dx = 0 if p == nx - 1 else 1

                @pl.when(more)
                def _():
                    start(face(s, 1 - slot, dx))

        @pl.when(more)
        def _():
            send_rest(s, 1 - slot)

    def injection():
        cells = cells_ref[...]
        count = cells.shape[1]
        i = lax.div(cells, total_y * total_z) - ix * nx
        j = lax.rem(lax.div(cells, total_z), total_y) - iy * ny
        k = lax.rem(cells, total_z) - iz * nz
        inside = (i >= 0) & (i < nx) & (j >= 0) & (j < ny)
        where = jnp.where(inside, i * ny + j, -1)
        rows = lax.broadcasted_iota(jnp.int32, (nx * ny, count), 0)
        spots = jnp.where(rows == where, 1.0, 0.0).astype(jnp.bfloat16)
        depth = lax.broadcasted_iota(jnp.int32, (nz, count), 0) == k
        nt = (((1,), (1,)), ((), ()))
        spread_lane = lax.broadcasted_iota(jnp.int32, (nz, count), 0)
        spread_rec = lax.rem(lax.broadcasted_iota(jnp.int32, (nz, count), 1), per)
        holder = lax.div(lax.broadcasted_iota(jnp.int32, (total_devices, count), 1), per)
        holder = holder == lax.broadcasted_iota(jnp.int32, (total_devices, count), 0)
        packed = R_all[:, 0, :]
        for m in range(STEPS):
            spread = jnp.where(spread_lane == m * per + spread_rec, 1.0, 0.0)
            found = jnp.dot(packed, spread, precision=lax.Precision.HIGHEST, preferred_element_type=F32)
            samples = jnp.sum(jnp.where(holder, found, 0.0), axis=0, keepdims=True)
            rest = jnp.where(depth, samples, 0.0)
            total = jnp.zeros((nx * ny, nz), F32)
            for _ in range(3):
                head = rest.astype(jnp.bfloat16)
                rest = rest - head.astype(F32)
                total = total + lax.dot_general(spots, head, nt, preferred_element_type=F32)
            inj[m] = total

    for s in range(2):
        loads[s].wait()
        start(face(s, 0, 0))
        start(face(s, 0, 1))
        send_rest(s, 0)
    gather = exchange(mine.at[0], R_all, g_send, g_recv)
    for s in range(2):
        loads[2 + s].wait()
        send_magnetic(s)
    loads[4].wait()
    loads[5].wait()
    for p in range(nx):
        lo = loss[p]
        keep[p] = (1.0 - lo) / (1.0 + lo)
        curl[p] = 0.5 / (perm[p] * (1.0 + lo))

    for s in range(2):
        for d in range(3):
            finish(first(s, d))
        update_h(s, 0, True)
    update_e(0, 0, 0)
    settle(gather)
    injection()
    update_e(1, 0, 0)

    def body(k, carry):
        slot = lax.rem(k, 2)
        for s in range(2):
            update_h(s, slot, False)
            update_e(s, k, slot)
        return carry

    lax.fori_loop(1, STEPS, body, 0)

    squares = jnp.zeros((ny, nz), F32)
    for p in range(nx):
        total = jnp.zeros((ny, nz), F32)
        for m in range(STEPS):
            n = STEPS - 1 - m
            total = total + (D[n, 0, p] * A[m, 0, p] + D[n, 1, p] * A[m, 1, p] + D[n, 2, p] * A[m, 2, p])
        g = -total / perm[p]
        grad[p] = g
        squares = squares + g * g
    part[0] = jnp.sum(squares, axis=0, keepdims=True)
    sums[pl.ds(me, 1)] = part[...]
    settle(exchange(part.at[0], sums, r_send, r_recv))
    tile = sums[:, 0, :]
    total = jnp.sum(jnp.sum(tile, axis=0, keepdims=True), axis=1, keepdims=True)
    rms = jnp.sqrt(total / (nx * ny * nz * gx * gy * gz) + 1e-06)
    rms_ref[...] = rms
    inverse = 1.0 / rms
    for p in range(nx):
        out_ref[p] = grad[p] * inverse


def per_device(
    permittivity, loss, fwd_electric, fwd_magnetic, adj_electric, adj_magnetic,
    wavelet, residuals, source_cell, receiver_cells, start_step,
):
    sizes = tuple(lax.axis_size(a) for a in ("gx", "gy", "gz"))
    gx, gy, gz = sizes
    nx, ny, nz = permittivity.shape
    devices = gx * gy * gz
    count = receiver_cells.shape[0]
    vmem = pl.BlockSpec(memory_space=pltpu.VMEM)
    hbm = pl.BlockSpec(memory_space=pltpu.HBM)
    dma = pltpu.SemaphoreType.DMA
    block = (nx, ny, nz)
    tall = ny + 16
    direction, rms = pl.pallas_call(
        functools.partial(kernel, sizes),
        out_shape=(
            pltpu.VMEM(block, F32),
            jax.ShapeDtypeStruct((1, 1), F32),
        ),
        in_specs=[hbm] * 11,
        out_specs=(vmem, vmem),
        scratch_shapes=[
            pltpu.VMEM((2, 3, nx, tall, nz), F32),
            pltpu.VMEM((2, 3, nx + 1, ny + 8, nz), F32),
            pltpu.VMEM(block, F32),
            pltpu.VMEM(block, F32),
            pltpu.VMEM(block, F32),
            pltpu.VMEM(block, F32),
            pltpu.VMEM((STEPS, 3) + block, F32),
            pltpu.VMEM((STEPS, 3) + block, F32),
            pltpu.VMEM((STEPS, nx * ny, nz), F32),
            pltpu.VMEM((devices, 1, nz), F32),
            pltpu.VMEM(block, F32),
            pltpu.VMEM((2, ny, nz), F32),
            pltpu.VMEM((2, 2, 3, tall, nz), F32),
            pltpu.VMEM((2, 2, 2, tall, nz), F32),
            pltpu.VMEM((2, 3, nx, nz), F32),
            pltpu.VMEM((2, 2, nx, nz), F32),
            pltpu.VMEM((2, 2, 3, nx, nz), F32),
            pltpu.VMEM((2, 2, 2, nx, nz), F32),
            pltpu.VMEM((2, ny, nz), F32),
            pltpu.VMEM((2, ny, nz), F32),
            pltpu.VMEM((2, 2, ny + 8, nz), F32),
            pltpu.VMEM((2, 2, ny + 8, nz), F32),
            pltpu.VMEM((2, 2, ny, nz), F32),
            pltpu.VMEM((2, 2, ny, nz), F32),
            pltpu.VMEM((2, 1, nz), F32),
            pltpu.VMEM((2, 1, nz), F32),
            pltpu.VMEM((2, 2, 1, nz), F32),
            pltpu.VMEM((2, 2, 1, nz), F32),
            pltpu.VMEM((2, 2, nx, nz), F32),
            pltpu.VMEM((2, 2, nx, nz), F32),
            pltpu.VMEM((2, ny, nz), F32),
            pltpu.VMEM((1, 1, nz), F32),
            pltpu.VMEM((devices, 1, nz), F32),
            pltpu.SMEM(wavelet.shape, F32),
            pltpu.SMEM((1,), jnp.int32),
            pltpu.SMEM((1,), jnp.int32),
            pltpu.VMEM((1, count), jnp.int32),
            pltpu.VMEM(residuals.shape, F32),
            pltpu.VMEM((1, 1, nz), F32),
            dma((11,)),
            dma((2, 12)),
            dma((2, 2, 12)),
            dma((2, 3)),
            dma((2, 3)),
            dma((devices,)),
            dma((devices,)),
            dma((devices,)),
            dma((devices,)),
        ],
        compiler_params=pltpu.CompilerParams(
            collective_id=0, has_side_effects=True, vmem_limit_bytes=60 * 1024 * 1024
        ),
    )(
        wavelet, source_cell, start_step, receiver_cells.reshape(1, count),
        permittivity, loss, fwd_electric, fwd_magnetic, adj_electric, adj_magnetic, residuals,
    )
    return direction, rms.reshape(())


def solution(mesh):
    block = P("gx", "gy", "gz")
    state = P(None, "gx", "gy", "gz")
    return jax.shard_map(
        per_device,
        mesh=mesh,
        in_specs=(
            block, block, state, state, state, state,
            P(), P(("gx", "gy", "gz"), None), P(), P(), P(),
        ),
        out_specs=(block, P()),
        check_vma=False,
    )
```

time: 44.5 us -> 37.2 us (0.84)
  Pallas kernels: 40.1 us -> 32.7 us
    pallas_call x1, Pallas kernels: 40.1 us -> 32.7 us  [per_device(): pl.pallas_call(functools.partial(kernel, sizes), out_shape=(pltpu.VMEM(bl...]
where the time goes in v1:
time: 37.2 us; the launch traced here: 37 us
  Pallas kernels  32.7 us (88%)
  between operations  3.62 us (10%)
  local copies, waits for them, and re-layouts  0.66 us (2%)
    pallas_call x1, Pallas kernels, per_device(): pl.pallas_call(functools.partial(kernel, sizes), out_shape=(pltpu.VMEM(bl...  32.7 us

profile of v1, /device:TPU:0, one launch (start us, length us, event | category | flops | bytes accessed | tf_op | source)
XLA Modules:
  0.0 37.0 jit_solution(9913805753861269394)
XLA Ops:
  1.9 32.7 %shard_map.122 = (f32[8,32,128]{2,1,0:T(8,128)S(1)}, f32[1,1]{1,0:T(1,128)}) custom-call(f32[64]{0:T(128)} %wav_hbm.1, s32[1]{0:T(128)S(6)} %copy.16.src_hbm, s32[1]{0:T(128)S(6)} %copy.17.start_hbm, s32[1,256]{1,0:T(1,128)} %bitcast.2, f32[8,32,128]{2,1,0:T(8,128)} %perm_hbm.1, f32[8,32,128]{2,1,0:T(8,128)} %loss_hbm.1, f32[3,8,32,128]{3,2,1,0:T(8,128)} %fe_hbm.1, ...), custom_call_target="tpu_custom_call" | custom-call | tf_op jit(solution)/shard_map/pallas_call | solution.py:507
  34.7 0.7 %copy.15 = f32[8,32,128]{2,1,0:T(8,128)} copy(f32[8,32,128]{2,1,0:T(8,128)S(1)} %get-tuple-element.6) | data formatting | bytes 262144

commit v2 on v1

v2 whole, which is shorter than its diff:
```python
import functools

import jax
import jax.numpy as jnp
from jax import lax
from jax.experimental import pallas as pl
from jax.experimental.pallas import tpu as pltpu
from jax.sharding import PartitionSpec as P

STEPS = 4
MESH = pl.DeviceIdType.MESH
F32 = jnp.float32
HALF = 0.5


def kernel(
    sizes,
    wav_hbm,
    src_hbm,
    start_hbm,
    cells_hbm,
    perm_hbm,
    loss_hbm,
    fe_hbm,
    fm_hbm,
    ae_hbm,
    am_hbm,
    res_hbm,
    out_ref,
    rms_ref,
    E,
    H,
    perm,
    loss,
    keep,
    curl,
    D,
    A,
    inj,
    spots,
    R_all,
    grad,
    HY,
    HP,
    xU,
    xD,
    ysU,
    ysD,
    yU,
    yD,
    yzU,
    yzD,
    zsU,
    zsD,
    zU,
    zD,
    zX,
    zXU,
    e1s,
    e2s,
    e1r,
    e2r,
    hys,
    hzs,
    part,
    sums,
    wav_ref,
    src_ref,
    start_ref,
    cells_ref,
    res_ref,
    mine,
    load_sem,
    f_send,
    f_recv,
    h_send,
    h_recv,
    g_send,
    g_recv,
    l_send,
    l_recv,
    r_send,
    r_recv,
):
    gx, gy, gz = sizes
    nx, ny, nz = perm.shape
    pad = H.shape[3] - ny
    own = slice(0, ny)
    above = slice(1, ny + 1)
    O = slice(pad, pad + ny)
    ix, iy, iz = lax.axis_index("gx"), lax.axis_index("gy"), lax.axis_index("gz")
    nplane = gx * gz
    spot = ix * gz + iz

    loads = [
        pltpu.make_async_copy(fe_hbm, E.at[0, :, :, own, :], load_sem.at[0]),
        pltpu.make_async_copy(ae_hbm, E.at[1, :, :, own, :], load_sem.at[1]),
        pltpu.make_async_copy(fm_hbm, H.at[0, :, 1 : nx + 1, O, :], load_sem.at[2]),
        pltpu.make_async_copy(am_hbm, H.at[1, :, 1 : nx + 1, O, :], load_sem.at[3]),
        pltpu.make_async_copy(loss_hbm, loss, load_sem.at[4]),
        pltpu.make_async_copy(perm_hbm, perm, load_sem.at[5]),
    ]
    small = [
        pltpu.make_async_copy(start_hbm, start_ref, load_sem.at[6]),
        pltpu.make_async_copy(res_hbm, res_ref, load_sem.at[7]),
        pltpu.make_async_copy(src_hbm, src_ref, load_sem.at[8]),
        pltpu.make_async_copy(wav_hbm, wav_ref, load_sem.at[9]),
        pltpu.make_async_copy(cells_hbm, cells_ref, load_sem.at[10]),
    ]
    for load in small:
        load.start()
    for load in loads:
        load.start()

    zero_plane = jnp.zeros((ny, nz), F32)
    zero_row = jnp.zeros((1, nz), F32)
    for s in range(2):
        for c in range(3):
            for p in range(nx):
                E[s, c, p, ny : ny + 1, :] = zero_row
        for c in (1, 2):
            H[s, c, 0, O, :] = zero_plane
    for buffer in (HY, HP, xU, xD, yU, yD, yzU, yzD, zU, zD, zX, zXU, e1r, e2r):
        buffer[...] = jnp.zeros(buffer.shape, F32)

    has = {
        "+x": ix < gx - 1, "-x": ix > 0, "+y": iy < gy - 1,
        "-y": iy > 0, "+z": iz < gz - 1, "-z": iz > 0,
    }
    flip = {"+": "-", "-": "+"}

    def route(steps):
        dev = [ix, iy, iz]
        size = (gx, gy, gz)
        can_send, can_recv = True, True
        for step in steps:
            axis = "xyz".index(step[1])
            dev[axis] = jnp.clip(dev[axis] + (1 if step[0] == "+" else -1), 0, size[axis] - 1)
            back = flip[step[0]] + step[1]
            can_send = has[step] if can_send is True else can_send & has[step]
            can_recv = has[back] if can_recv is True else can_recv & has[back]
        return tuple(dev), can_send, can_recv

    layer = []
    for d in range(1, nplane):
        q = lax.rem(spot + d, nplane)
        layer.append((q, (q // gz, iy, lax.rem(q, gz))))
    line = []
    for d in range(1, gy):
        q = lax.rem(iy + d, gy)
        line.append((q, (ix, q, iz)))
    barrier = pltpu.get_barrier_semaphore()
    greeted = len(layer) + len(line)
    for steps in (("+x", "-y"), ("-x", "+y"), ("+y", "-z"), ("-y", "+z")):
        dev, can_send, _ = route(steps)
        greeted = greeted + can_send.astype(jnp.int32)

        @pl.when(can_send)
        def _():
            pl.semaphore_signal(barrier, inc=1, device_id=dev, device_id_type=MESH)

    for _, dev in layer + line:
        pl.semaphore_signal(barrier, inc=1, device_id=dev, device_id_type=MESH)

    lane = lax.broadcasted_iota(jnp.int32, (ny, nz), 1)
    row = lax.broadcasted_iota(jnp.int32, (ny, nz), 0)
    lane_p = lax.broadcasted_iota(jnp.int32, (nx, nz), 1)
    row_p = lax.broadcasted_iota(jnp.int32, (nx, nz), 0)

    per, trace = res_hbm.shape
    small[0].wait()
    small[1].wait()
    begin = start_ref[0]
    time_at = lax.broadcasted_iota(jnp.int32, (trace, nz), 0)
    turn = lax.div(lax.broadcasted_iota(jnp.int32, (trace, nz), 1), per)
    pick = jnp.where(time_at == begin + STEPS - 1 - turn, 1.0, 0.0)
    found = jnp.dot(res_ref[...], pick, precision=lax.Precision.HIGHEST, preferred_element_type=F32)
    mask = lax.rem(lax.broadcasted_iota(jnp.int32, (per, nz), 1), per)
    mask = mask == lax.broadcasted_iota(jnp.int32, (per, nz), 0)
    mine[0] = jnp.sum(jnp.where(mask, found, 0.0), axis=0, keepdims=True)
    R_all[pl.ds(iy * nplane + spot, 1)] = mine[...]
    for load in small[2:]:
        load.wait()
    pl.semaphore_wait(barrier, greeted)

    def remote(src, dst, ssem, rsem, dev):
        return pltpu.make_async_remote_copy(
            src_ref=src, dst_ref=dst, send_sem=ssem, recv_sem=rsem,
            device_id=dev, device_id_type=MESH,
        )

    def exchange(peers, at, src, slots, send_sems, recv_sems):
        copies = []
        for d, (q, dev) in enumerate(peers):
            send = remote(src, slots(at), send_sems.at[d], recv_sems.at[at], dev)
            recv = remote(src, slots(q), send_sems.at[d], recv_sems.at[q], dev)
            send.start()
            copies.append((send, recv))
        return copies

    def settle(copies):
        for send, recv in copies:
            recv.wait_recv()
        for send, recv in copies:
            send.wait_send()

    def face(s, slot, d):
        table = (
            (("+x",), E.at[s, :, nx - 1, own, :], xU.at[slot, s, :, own, :]),
            (("-x",), E.at[s, 1:3, 0, own, :], xD.at[slot, s]),
            (("+y",), ysU.at[s], yU.at[slot, s, :, 0:nx, :]),
            (("-y",), ysD.at[s], yD.at[slot, s]),
            (("+z",), zsU.at[s], zU.at[slot, s, own, :]),
            (("-z",), zsD.at[s], zD.at[slot, s]),
            (("+x", "-y"), e1s.at[s], e1r.at[slot, s]),
            (("-x", "+y"), e2s.at[s], e2r.at[slot, s]),
            (("+x", "-z"), E.at[s, 0, nx - 1, own, :], zX.at[slot, s]),
            (("-x", "+z"), E.at[s, 2, 0, own, :], zXU.at[slot, s]),
            (("+y", "-z"), ysU.at[s, 1], yzU.at[slot, s]),
            (("-y", "+z"), ysD.at[s, 1], yzD.at[slot, s]),
        )
        steps, source, target = table[d]
        dev, can_send, can_recv = route(steps)
        return remote(source, target, f_send.at[s, d], f_recv.at[slot, s, d], dev), can_send, can_recv

    def first(s, d):
        table = (
            (("+x",), H.at[s, 1:3, nx, O, :], H.at[s, 1:3, 0, O, :]),
            (("+y",), hys.at[s], HY.at[s]),
            (("+z",), hzs.at[s], HP.at[s]),
        )
        steps, source, target = table[d]
        dev, can_send, can_recv = route(steps)
        return remote(source, target, h_send.at[s, d], h_recv.at[s, d], dev), can_send, can_recv

    def start(item, extra=None):
        copy, can_send, _ = item

        @pl.when(can_send if extra is None else can_send & extra)
        def _():
            copy.start()

    def finish(item):
        copy, can_send, _ = item

        @pl.when(can_send)
        def _():
            copy.wait_send()

    def arrive(item):
        copy, _, can_recv = item

        @pl.when(can_recv)
        def _():
            copy.wait_recv()

    def pack_column(acc, value, source, j):
        return jnp.where(lane == j, pltpu.roll(value, (j - source) % nz, 1), acc)

    def up_z(value, halo, j):
        return jnp.where(lane == nz - 1, pltpu.roll(halo, (nz - 1 - j) % nz, 1), pltpu.roll(value, nz - 1, 1))

    def down_z(value, halo, j):
        rolled = pltpu.roll(value, 1, 1)
        return jnp.where(lane == 0, pltpu.roll(halo, (nz - j) % nz, 1), rolled)

    def pack_rows(s, p, ex, ey, ez):
        ysU[s, 0, p : p + 1, :] = ex[ny - 1 : ny, :]
        ysU[s, 1, p : p + 1, :] = ey[ny - 1 : ny, :]
        ysU[s, 2, p : p + 1, :] = ez[ny - 1 : ny, :]
        ysD[s, 0, p : p + 1, :] = ex[0:1, :]
        ysD[s, 1, p : p + 1, :] = ez[0:1, :]
        if p == nx - 1:
            e1s[s] = ex[0:1, :]
        if p == 0:
            e2s[s] = ey[ny - 1 : ny, :]

    def pack_low(s):
        acc = jnp.zeros((ny, nz), F32)
        for p in range(nx):
            acc = pack_column(acc, E[s, 0, p, own, :], 0, p)
            acc = pack_column(acc, E[s, 1, p, own, :], 0, nx + p)
        zsD[s] = acc

    def pack_high(s):
        acc = jnp.zeros((ny, nz), F32)
        for p in range(nx):
            acc = pack_column(acc, E[s, 0, p, own, :], nz - 1, p)
            acc = pack_column(acc, E[s, 1, p, own, :], nz - 1, nx + p)
            acc = pack_column(acc, E[s, 2, p, own, :], nz - 1, 2 * nx + p)
        zsU[s] = acc

    def send_z(s, slot, extra=None):
        for sign, pack, d in (("-z", pack_low, 5), ("+z", pack_high, 4)):
            @pl.when(has[sign] if extra is None else has[sign] & extra)
            def _():
                pack(s)
                face(s, slot, d)[0].start()

    def send_first(s):
        for d in (8, 9, 0, 1):
            start(face(s, 0, d))
        for p in range(nx):
            pack_rows(s, p, E[s, 0, p, own, :], E[s, 1, p, own, :], E[s, 2, p, own, :])
        for d in (10, 11, 6, 7, 2, 3):
            start(face(s, 0, d))
        send_z(s, 0)

    def send_magnetic(s):
        start(first(s, 0))
        for p in range(nx):
            hys[s, 0, p : p + 1, :] = H[s, 0, p + 1, pad + ny - 1 : pad + ny, :]
            hys[s, 1, p : p + 1, :] = H[s, 2, p + 1, pad + ny - 1 : pad + ny, :]
        start(first(s, 1))

        @pl.when(has["+z"])
        def _():
            acc = jnp.zeros((ny, nz), F32)
            for p in range(nx):
                acc = pack_column(acc, H[s, 1, p + 1, O, :], nz - 1, p)
                acc = pack_column(acc, H[s, 0, p + 1, O, :], nz - 1, nx + p)
            hzs[s] = acc
            first(s, 2)[0].start()

    half_x = jnp.where(has["-x"], HALF, 0.0)
    half_y = jnp.where(has["-y"], HALF, 0.0)

    def update_h(s, slot, opening):
        for d in (3, 5):
            arrive(face(s, slot, d))
        for p in range(nx):
            E[s, 0, p, ny : ny + 1, :] = yD[slot, s, 0, p : p + 1, :]
            E[s, 2, p, ny : ny + 1, :] = yD[slot, s, 1, p : p + 1, :]
        halo = zD[slot, s]
        for p in range(nx):
            if p == nx - 1:
                for d in (0, 1):
                    arrive(face(s, slot, d))
                next_y, next_z = xD[slot, s, 0], xD[slot, s, 1]
            else:
                next_y, next_z = E[s, 1, p + 1, own, :], E[s, 2, p + 1, own, :]
            ex, ey, ez = E[s, 0, p, own, :], E[s, 1, p, own, :], E[s, 2, p, own, :]
            hx = H[s, 0, p + 1, O, :] - HALF * (E[s, 2, p, above, :] - ez - (up_z(ey, halo, nx + p) - ey))
            hy = H[s, 1, p + 1, O, :] - HALF * (up_z(ex, halo, p) - ex - (next_z - ez))
            hz = H[s, 2, p + 1, O, :] - HALF * (next_y - ey - (E[s, 0, p, above, :] - ex))
            H[s, 0, p + 1, O, :] = hx
            H[s, 1, p + 1, O, :] = hy
            H[s, 2, p + 1, O, :] = hz
        for d in (2, 6, 7, 8, 10):
            arrive(face(s, slot, d))
        if opening:
            arrive(first(s, 0))
            arrive(first(s, 1))
        xU[slot, s, 0, ny : ny + 1, :] = e1r[slot, s]
        yU[slot, s, 1, nx : nx + 1, :] = e2r[slot, s]
        ex, ey, ez = xU[slot, s, 0, own, :], xU[slot, s, 1, own, :], xU[slot, s, 2, own, :]
        side_y = H[s, 1, 0, O, :] - half_x * (up_z(ex, zX[slot, s], 0) - ex - (E[s, 2, 0, own, :] - ez))
        side_z = H[s, 2, 0, O, :] - half_x * (E[s, 1, 0, own, :] - ey - (xU[slot, s, 0, above, :] - ex))
        H[s, 1, 0, O, :] = side_y
        H[s, 2, 0, O, :] = side_z
        ex, ey, ez = yU[slot, s, 0, 0:nx, :], yU[slot, s, 1, 0:nx, :], yU[slot, s, 2, 0:nx, :]
        far = jnp.where(lane_p == nz - 1, pltpu.roll(yzU[slot, s], nz - 1, 1), pltpu.roll(ey, nz - 1, 1))
        hx = HY[s, 0] - half_y * (ysD[s, 1] - ez - (far - ey))
        hz = HY[s, 1] - half_y * (yU[slot, s, 1, 1 : nx + 1, :] - ey - (ysD[s, 0] - ex))
        HY[s, 0] = hx
        HY[s, 1] = hz
        for p in range(nx):
            H[s, 0, p + 1, pad - 1 : pad, :] = hx[p : p + 1, :]
            H[s, 2, p + 1, pad - 1 : pad, :] = hz[p : p + 1, :]
        for d in (4, 9, 11):
            arrive(face(s, slot, d))
        if opening:
            arrive(first(s, 2))

        @pl.when(has["-z"])
        def _():
            edge = jnp.broadcast_to(yzD[slot, s, :, nz - 1 : nz], (nx, nz))
            edge = jnp.where(lane_p == 2 * nx + row_p, edge, 0.0)
            zU[slot, s, ny : ny + 1, :] = jnp.sum(edge, axis=0, keepdims=True)
            below = zU[slot, s, own, :]
            wide = jnp.where(lane == 3 * nx, pltpu.roll(zXU[slot, s], (3 * nx + 1) % nz, 1), below)
            along = pltpu.roll(pltpu.roll(wide, nz - 1, 1) - wide, nz - 2 * nx, 1)
            across = pltpu.roll(zU[slot, s, above, :] - below, nz - nx, 1)
            change = jnp.where(lane < nx, along, across)
            HP[s] = HP[s] - jnp.where(lane < nx, HALF, -HALF) * (zsD[s] - below - change)

    src = src_ref[0]
    total_z, total_y = nz * gz, ny * gy
    src_i = lax.div(src, total_y * total_z) - ix * nx
    src_j = lax.rem(lax.div(src, total_z), total_y) - iy * ny
    src_k = lax.rem(src, total_z) - iz * nz
    src_mask = (row == src_j) & (lane == src_k)

    def update_e(s, k, slot):
        for d in range(12):
            finish(face(s, slot, d))
        more = k < STEPS - 1
        halo = HP[s]
        below = slice(pad - 1, pad + ny - 1)
        pulse = wav_ref[begin + k]
        for p in (nx - 1,) + tuple(range(nx - 1)):
            hx, hy, hz = H[s, 0, p + 1, O, :], H[s, 1, p + 1, O, :], H[s, 2, p + 1, O, :]
            kp, cl = keep[p], curl[p]
            ox, oy, oz = E[s, 0, p, own, :], E[s, 1, p, own, :], E[s, 2, p, own, :]
            ex = kp * ox + cl * (hz - H[s, 2, p + 1, below, :] - (hy - down_z(hy, halo, p)))
            ey = kp * oy + cl * (hx - down_z(hx, halo, nx + p) - (hz - H[s, 2, p, O, :]))
            ez = kp * oz + cl * (hy - H[s, 1, p, O, :] - (hx - H[s, 0, p + 1, below, :]))
            if s == 0:
                ez = ez + jnp.where(src_mask, jnp.where(src_i == p, pulse, 0.0), 0.0)
                D[k, 0, p] = ex - ox
                D[k, 1, p] = ey - oy
                D[k, 2, p] = ez - oz
            else:
                ez = ez + inj[k, p * ny : (p + 1) * ny, :]
                A[k, 0, p] = ex
                A[k, 1, p] = ey
                A[k, 2, p] = ez
            E[s, 0, p, own, :] = ex
            E[s, 1, p, own, :] = ey
            E[s, 2, p, own, :] = ez
            pack_rows(s, p, ex, ey, ez)
            if p == nx - 1:
                for d in (6, 8, 0):
                    start(face(s, 1 - slot, d), more)
            if p == 0:
                for d in (7, 9, 1):
                    start(face(s, 1 - slot, d), more)
        for d in (10, 11, 2, 3):
            start(face(s, 1 - slot, d), more)
        send_z(s, 1 - slot, more)

    count = cells_ref.shape[1]

    def place_cells():
        cells = cells_ref[...]
        i = lax.div(cells, total_y * total_z) - ix * nx
        j = lax.rem(lax.div(cells, total_z), total_y) - iy * ny
        inside = (i >= 0) & (i < nx) & (j >= 0) & (j < ny)
        where = jnp.where(inside, i * ny + j, -1)
        rows = lax.broadcasted_iota(jnp.int32, (nx * ny, count), 0)
        spots[...] = jnp.where(rows == where, 1.0, 0.0).astype(jnp.bfloat16)

    def inject(m):
        k = lax.rem(cells_ref[...], total_z) - iz * nz
        depth = lax.broadcasted_iota(jnp.int32, (nz, count), 0) == k
        nt = (((1,), (1,)), ((), ()))
        spread_lane = lax.broadcasted_iota(jnp.int32, (nz, count), 0)
        spread_rec = lax.rem(lax.broadcasted_iota(jnp.int32, (nz, count), 1), per)
        device = lax.div(lax.broadcasted_iota(jnp.int32, (gy * nplane, count), 1), per)
        at_x, at_y, at_z = device // (gy * gz), lax.rem(device // gz, gy), lax.rem(device, gz)
        holder = at_y * nplane + at_x * gz + at_z == lax.broadcasted_iota(jnp.int32, (gy * nplane, count), 0)
        spread = jnp.where(spread_lane == m * per + spread_rec, 1.0, 0.0)
        found = jnp.dot(R_all[:, 0, :], spread, precision=lax.Precision.HIGHEST, preferred_element_type=F32)
        samples = jnp.sum(jnp.where(holder, found, 0.0), axis=0, keepdims=True)
        rest = jnp.where(depth, samples, 0.0)
        total = jnp.zeros((nx * ny, nz), F32)
        for _ in range(3):
            head = rest.astype(jnp.bfloat16)
            rest = rest - head.astype(F32)
            total = total + lax.dot_general(spots[...], head, nt, preferred_element_type=F32)
        inj[m] = total

    gather = exchange(layer, spot, mine.at[0], lambda q: R_all.at[iy * nplane + q], g_send, g_recv)
    for s in range(2):
        loads[s].wait()
        send_first(s)
    for s in range(2):
        loads[2 + s].wait()
        send_magnetic(s)
    loads[4].wait()
    loads[5].wait()
    for p in range(nx):
        lo = loss[p]
        keep[p] = (1.0 - lo) / (1.0 + lo)
        curl[p] = 0.5 / (perm[p] * (1.0 + lo))
    settle(gather)
    block = R_all.at[pl.ds(iy * nplane, nplane)]
    gather = exchange(line, iy, block, lambda q: R_all.at[pl.ds(q * nplane, nplane)], l_send, l_recv)
    place_cells()

    for s in range(2):
        for d in range(3):
            finish(first(s, d))
        update_h(s, 0, True)
    update_e(0, 0, 0)
    settle(gather)
    inject(0)
    update_e(1, 0, 0)
    inject(1)

    def body(k, carry):
        slot = lax.rem(k, 2)
        for s in range(2):
            update_h(s, slot, False)
            update_e(s, k, slot)

        @pl.when(k < STEPS - 1)
        def _():
            inject(k + 1)

        return carry

    lax.fori_loop(1, STEPS, body, 0)

    squares = jnp.zeros((ny, nz), F32)
    for p in range(nx):
        total = jnp.zeros((ny, nz), F32)
        for m in range(STEPS):
            n = STEPS - 1 - m
            total = total + (D[n, 0, p] * A[m, 0, p] + D[n, 1, p] * A[m, 1, p] + D[n, 2, p] * A[m, 2, p])
        g = -total / perm[p]
        grad[p] = g
        squares = squares + g * g
    part[0] = jnp.sum(squares, axis=0, keepdims=True)
    devices = gy * nplane
    me = iy * nplane + spot
    peers = []
    for d in range(1, devices):
        q = lax.rem(me + d, devices)
        peers.append((q, (lax.rem(q // gz, gx), q // nplane, lax.rem(q, gz))))
    sums[pl.ds(me, 1)] = part[...]
    settle(exchange(peers, me, part.at[0], lambda q: sums.at[q], r_send, r_recv))
    tile = sums[:, 0, :]
    total = jnp.sum(jnp.sum(tile, axis=0, keepdims=True), axis=1, keepdims=True)
    rms = jnp.sqrt(total / (nx * ny * nz * gx * gy * gz) + 1e-06)
    rms_ref[...] = rms
    inverse = 1.0 / rms
    for p in range(nx):
        out_ref[p] = grad[p] * inverse


def per_device(
    permittivity, loss, fwd_electric, fwd_magnetic, adj_electric, adj_magnetic,
    wavelet, residuals, source_cell, receiver_cells, start_step,
):
    sizes = tuple(lax.axis_size(a) for a in ("gx", "gy", "gz"))
    gx, gy, gz = sizes
    nx, ny, nz = permittivity.shape
    devices = gx * gy * gz
    count = receiver_cells.shape[0]
    vmem = pl.BlockSpec(memory_space=pltpu.VMEM)
    hbm = pl.BlockSpec(memory_space=pltpu.HBM)
    dma = pltpu.SemaphoreType.DMA
    block = (nx, ny, nz)

    def room(*shape):
        return pltpu.VMEM(shape, F32)

    direction, rms = pl.pallas_call(
        functools.partial(kernel, sizes),
        out_shape=(
            pltpu.VMEM(block, F32),
            jax.ShapeDtypeStruct((1, 1), F32),
        ),
        in_specs=[hbm] * 11,
        out_specs=(vmem, vmem),
        scratch_shapes=[
            room(2, 3, nx, ny + 8, nz),
            room(2, 3, nx + 1, ny + 8, nz),
            room(*block),
            room(*block),
            room(*block),
            room(*block),
            room(STEPS, 3, *block),
            room(STEPS, 3, *block),
            room(STEPS, nx * ny, nz),
            pltpu.VMEM((nx * ny, count), jnp.bfloat16),
            room(devices, 1, nz),
            room(*block),
            room(2, 2, nx, nz),
            room(2, ny, nz),
            room(2, 2, 3, ny + 8, nz),
            room(2, 2, 2, ny, nz),
            room(2, 3, nx, nz),
            room(2, 2, nx, nz),
            room(2, 2, 3, nx + 8, nz),
            room(2, 2, 2, nx, nz),
            room(2, 2, nx, nz),
            room(2, 2, nx, nz),
            room(2, ny, nz),
            room(2, ny, nz),
            room(2, 2, ny + 8, nz),
            room(2, 2, ny, nz),
            room(2, 2, ny, nz),
            room(2, 2, ny, nz),
            room(2, 1, nz),
            room(2, 1, nz),
            room(2, 2, 1, nz),
            room(2, 2, 1, nz),
            room(2, 2, nx, nz),
            room(2, ny, nz),
            room(1, 1, nz),
            room(devices, 1, nz),
            pltpu.SMEM(wavelet.shape, F32),
            pltpu.SMEM((1,), jnp.int32),
            pltpu.SMEM((1,), jnp.int32),
            pltpu.VMEM((1, count), jnp.int32),
            room(*residuals.shape),
            room(1, 1, nz),
            dma((11,)),
            dma((2, 12)),
            dma((2, 2, 12)),
            dma((2, 3)),
            dma((2, 3)),
            dma((gx * gz,)),
            dma((gx * gz,)),
            dma((gy,)),
            dma((gy,)),
            dma((devices,)),
            dma((devices,)),
        ],
        compiler_params=pltpu.CompilerParams(
            collective_id=0, has_side_effects=True, vmem_limit_bytes=60 * 1024 * 1024
        ),
    )(
        wavelet, source_cell, start_step, receiver_cells.reshape(1, count),
        permittivity, loss, fwd_electric, fwd_magnetic, adj_electric, adj_magnetic, residuals,
    )
    return direction, rms.reshape(())


def solution(mesh):
    block = P("gx", "gy", "gz")
    state = P(None, "gx", "gy", "gz")
    return jax.shard_map(
        per_device,
        mesh=mesh,
        in_specs=(
            block, block, state, state, state, state,
            P(), P(("gx", "gy", "gz"), None), P(), P(), P(),
        ),
        out_specs=(block, P()),
        check_vma=False,
    )
```

time: 37.2 us -> 35.9 us (0.965)
  Pallas kernels: 32.7 us -> 31.4 us
    pallas_call x1, Pallas kernels: 32.7 us -> 31.4 us  [per_device(): pl.pallas_call(functools.partial(kernel, sizes), out_shape=(pltpu.VMEM(bl...]
where the time goes in v2:
time: 35.9 us; the launch traced here: 35.7 us
  Pallas kernels  31.4 us (87%)
  between operations  3.62 us (10%)
  local copies, waits for them, and re-layouts  0.66 us (2%)
    pallas_call x1, Pallas kernels, per_device(): pl.pallas_call(functools.partial(kernel, sizes), out_shape=(pltpu.VMEM(bl...  31.4 us

profile of v2, /device:TPU:0, one launch (start us, length us, event | category | flops | bytes accessed | tf_op | source)
XLA Modules:
  0.0 35.7 jit_solution(288353133622024944)
XLA Ops:
  1.9 31.4 %shard_map.122 = (f32[8,32,128]{2,1,0:T(8,128)S(1)}, f32[1,1]{1,0:T(1,128)}) custom-call(f32[64]{0:T(128)} %wav_hbm.1, s32[1]{0:T(128)S(6)} %copy.16.src_hbm, s32[1]{0:T(128)S(6)} %copy.17.start_hbm, s32[1,256]{1,0:T(1,128)} %bitcast.2, f32[8,32,128]{2,1,0:T(8,128)} %perm_hbm.1, f32[8,32,128]{2,1,0:T(8,128)} %loss_hbm.1, f32[3,8,32,128]{3,2,1,0:T(8,128)} %fe_hbm.1, ...), custom_call_target="tpu_custom_call" | custom-call | tf_op jit(solution)/shard_map/pallas_call | solution.py:549
  33.3 0.7 %copy.15 = f32[8,32,128]{2,1,0:T(8,128)} copy(f32[8,32,128]{2,1,0:T(8,128)S(1)} %get-tuple-element.6) | data formatting | bytes 262144

commit v3 on v2

--- a/solution.py
+++ b/solution.py
@@ -37,7 +37,10 @@
     D,
     A,
     inj,
+    late,
+    late_z,
     spots,
+    spots_z,
     R_all,
     grad,
     HY,
@@ -325,18 +328,37 @@
     half_x = jnp.where(has["-x"], HALF, 0.0)
     half_y = jnp.where(has["-y"], HALF, 0.0)
 
-    def update_h(s, slot, opening):
+    base = nx * ny
+    rim = base + 2 * ny + 2 * nx
+
+    def add_late(slot):
+        for d in range(12):
+            finish(face(1, slot, d))
+        for p in range(nx):
+            extra = late[p * ny : (p + 1) * ny, :]
+            E[1, 2, p, own, :] = E[1, 2, p, own, :] + extra
+            A[0, 2, p] = A[0, 2, p] + extra
+
+    def update_h(s, slot, opening, behind=False):
+        if behind:
+            add_late(slot)
         for d in (3, 5):
             arrive(face(s, slot, d))
         for p in range(nx):
             E[s, 0, p, ny : ny + 1, :] = yD[slot, s, 0, p : p + 1, :]
-            E[s, 2, p, ny : ny + 1, :] = yD[slot, s, 1, p : p + 1, :]
+            if behind:
+                at = base + 2 * ny + nx + p
+                E[s, 2, p, ny : ny + 1, :] = yD[slot, s, 1, p : p + 1, :] + late[at : at + 1, :]
+            else:
+                E[s, 2, p, ny : ny + 1, :] = yD[slot, s, 1, p : p + 1, :]
         halo = zD[slot, s]
         for p in range(nx):
             if p == nx - 1:
                 for d in (0, 1):
                     arrive(face(s, slot, d))
                 next_y, next_z = xD[slot, s, 0], xD[slot, s, 1]
+                if behind:
+                    next_z = next_z + late[base + ny : base + 2 * ny, :]
             else:
                 next_y, next_z = E[s, 1, p + 1, own, :], E[s, 2, p + 1, own, :]
             ex, ey, ez = E[s, 0, p, own, :], E[s, 1, p, own, :], E[s, 2, p, own, :]
@@ -354,13 +376,19 @@
         xU[slot, s, 0, ny : ny + 1, :] = e1r[slot, s]
         yU[slot, s, 1, nx : nx + 1, :] = e2r[slot, s]
         ex, ey, ez = xU[slot, s, 0, own, :], xU[slot, s, 1, own, :], xU[slot, s, 2, own, :]
+        if behind:
+            ez = ez + late[base : base + ny, :]
         side_y = H[s, 1, 0, O, :] - half_x * (up_z(ex, zX[slot, s], 0) - ex - (E[s, 2, 0, own, :] - ez))
         side_z = H[s, 2, 0, O, :] - half_x * (E[s, 1, 0, own, :] - ey - (xU[slot, s, 0, above, :] - ex))
         H[s, 1, 0, O, :] = side_y
         H[s, 2, 0, O, :] = side_z
         ex, ey, ez = yU[slot, s, 0, 0:nx, :], yU[slot, s, 1, 0:nx, :], yU[slot, s, 2, 0:nx, :]
         far = jnp.where(lane_p == nz - 1, pltpu.roll(yzU[slot, s], nz - 1, 1), pltpu.roll(ey, nz - 1, 1))
-        hx = HY[s, 0] - half_y * (ysD[s, 1] - ez - (far - ey))
+        near = ysD[s, 1]
+        if behind:
+            ez = ez + late[base + 2 * ny : base + 2 * ny + nx, :]
+            near = near + late[rim : rim + nx, :]
+        hx = HY[s, 0] - half_y * (near - ez - (far - ey))
         hz = HY[s, 1] - half_y * (yU[slot, s, 1, 1 : nx + 1, :] - ey - (ysD[s, 0] - ex))
         HY[s, 0] = hx
         HY[s, 1] = hz
@@ -374,13 +402,18 @@
 
         @pl.when(has["-z"])
         def _():
-            edge = jnp.broadcast_to(yzD[slot, s, :, nz - 1 : nz], (nx, nz))
-            edge = jnp.where(lane_p == 2 * nx + row_p, edge, 0.0)
-            zU[slot, s, ny : ny + 1, :] = jnp.sum(edge, axis=0, keepdims=True)
+            edge, far_x = yzD[slot, s], zXU[slot, s]
+            if behind:
+                edge = edge + late_z[ny : ny + nx, :]
+                far_x = far_x + late_z[0:ny, :]
+                zU[slot, s, own, :] = zU[slot, s, own, :] + late_z[0:ny, :]
+            edge = jnp.broadcast_to(edge[:, nz - 1 : nz], (nx, nz))
+            edge = jnp.sum(jnp.where(lane_p == nx + row_p, edge, 0.0), axis=0, keepdims=True)
             below = zU[slot, s, own, :]
-            wide = jnp.where(lane == 3 * nx, pltpu.roll(zXU[slot, s], (3 * nx + 1) % nz, 1), below)
-            along = pltpu.roll(pltpu.roll(wide, nz - 1, 1) - wide, nz - 2 * nx, 1)
-            across = pltpu.roll(zU[slot, s, above, :] - below, nz - nx, 1)
+            next_i = jnp.where(lane == nx - 1, pltpu.roll(far_x, nx, 1), pltpu.roll(below, nz - 2 * nx - 1, 1))
+            next_j = jnp.where(row == ny - 1, edge, pltpu.roll(zU[slot, s, above, :], nz - nx, 1))
+            along = next_i - pltpu.roll(below, nz - 2 * nx, 1)
+            across = next_j - pltpu.roll(below, nz - nx, 1)
             change = jnp.where(lane < nx, along, across)
             HP[s] = HP[s] - jnp.where(lane < nx, HALF, -HALF) * (zsD[s] - below - change)
 
@@ -391,9 +424,10 @@
     src_k = lax.rem(src, total_z) - iz * nz
     src_mask = (row == src_j) & (lane == src_k)
 
-    def update_e(s, k, slot):
-        for d in range(12):
-            finish(face(s, slot, d))
+    def update_e(s, k, slot, behind=False):
+        if not behind:
+            for d in range(12):
+                finish(face(s, slot, d))
         more = k < STEPS - 1
         halo = HP[s]
         below = slice(pad - 1, pad + ny - 1)
@@ -411,7 +445,8 @@
                 D[k, 1, p] = ey - oy
                 D[k, 2, p] = ez - oz
             else:
-                ez = ez + inj[k, p * ny : (p + 1) * ny, :]
+                if not (isinstance(k, int) and k == 0):
+                    ez = ez + inj[k, p * ny : (p + 1) * ny, :]
                 A[k, 0, p] = ex
                 A[k, 1, p] = ey
                 A[k, 2, p] = ez
@@ -435,15 +470,24 @@
         cells = cells_ref[...]
         i = lax.div(cells, total_y * total_z) - ix * nx
         j = lax.rem(lax.div(cells, total_z), total_y) - iy * ny
-        inside = (i >= 0) & (i < nx) & (j >= 0) & (j < ny)
-        where = jnp.where(inside, i * ny + j, -1)
-        rows = lax.broadcasted_iota(jnp.int32, (nx * ny, count), 0)
-        spots[...] = jnp.where(rows == where, 1.0, 0.0).astype(jnp.bfloat16)
-
-    def inject(m):
-        k = lax.rem(cells_ref[...], total_z) - iz * nz
-        depth = lax.broadcasted_iota(jnp.int32, (nz, count), 0) == k
-        nt = (((1,), (1,)), ((), ()))
+        k = lax.rem(cells, total_z) - iz * nz
+        in_x, in_y = (i >= 0) & (i < nx), (j >= 0) & (j < ny)
+        where = jnp.where(in_x & in_y, i * ny + j, -1)
+        where = jnp.where((i == -1) & in_y, base + j, where)
+        where = jnp.where((i == nx) & in_y, base + ny + j, where)
+        where = jnp.where((j == -1) & in_x, base + 2 * ny + i, where)
+        where = jnp.where((j == ny) & in_x, base + 2 * ny + nx + i, where)
+        again = jnp.where((j == 0) & in_x, rim + i, -1)
+        rows = lax.broadcasted_iota(jnp.int32, spots.shape, 0)
+        spots[...] = jnp.where((rows == where) | (rows == again), 1.0, 0.0).astype(jnp.bfloat16)
+        where = jnp.where(in_y & (i >= 0) & (i <= nx) & (k == -1), j, -1)
+        where = jnp.where((j == ny) & in_x & (k == -1), ny + i, where)
+        rows = lax.broadcasted_iota(jnp.int32, spots_z.shape, 0)
+        spots_z[...] = jnp.where(rows == where, 1.0, 0.0).astype(jnp.bfloat16)
+
+    nt = (((1,), (1,)), ((), ()))
+
+    def sampled(m):
         spread_lane = lax.broadcasted_iota(jnp.int32, (nz, count), 0)
         spread_rec = lax.rem(lax.broadcasted_iota(jnp.int32, (nz, count), 1), per)
         device = lax.div(lax.broadcasted_iota(jnp.int32, (gy * nplane, count), 1), per)
@@ -451,14 +495,31 @@
         holder = at_y * nplane + at_x * gz + at_z == lax.broadcasted_iota(jnp.int32, (gy * nplane, count), 0)
         spread = jnp.where(spread_lane == m * per + spread_rec, 1.0, 0.0)
         found = jnp.dot(R_all[:, 0, :], spread, precision=lax.Precision.HIGHEST, preferred_element_type=F32)
-        samples = jnp.sum(jnp.where(holder, found, 0.0), axis=0, keepdims=True)
-        rest = jnp.where(depth, samples, 0.0)
-        total = jnp.zeros((nx * ny, nz), F32)
+        return jnp.sum(jnp.where(holder, found, 0.0), axis=0, keepdims=True)
+
+    def spread_out(rows, rest):
+        total = jnp.zeros((rows.shape[0], nz), F32)
         for _ in range(3):
             head = rest.astype(jnp.bfloat16)
             rest = rest - head.astype(F32)
-            total = total + lax.dot_general(spots[...], head, nt, preferred_element_type=F32)
-        inj[m] = total
+            total = total + lax.dot_general(rows, head, nt, preferred_element_type=F32)
+        return total
+
+    lane_c = lax.broadcasted_iota(jnp.int32, (nz, count), 0)
+
+    def inject(m):
+        k = lax.rem(cells_ref[...], total_z) - iz * nz
+        inj[m] = spread_out(spots[0:base, :], jnp.where(lane_c == k, sampled(m), 0.0))
+
+    def inject_late():
+        cells = cells_ref[...]
+        k = lax.rem(cells, total_z) - iz * nz
+        i = lax.div(cells, total_y * total_z) - ix * nx
+        samples = sampled(0)
+        late[...] = spread_out(spots[...], jnp.where(lane_c == k, samples, 0.0))
+        j = lax.rem(lax.div(cells, total_z), total_y) - iy * ny
+        at = jnp.where((i == nx) | (j == ny), nz - 1, 2 * nx + i)
+        late_z[...] = spread_out(spots_z[...], jnp.where(lane_c == at, samples, 0.0))
 
     gather = exchange(layer, spot, mine.at[0], lambda q: R_all.at[iy * nplane + q], g_send, g_recv)
     for s in range(2):
@@ -483,10 +544,15 @@
             finish(first(s, d))
         update_h(s, 0, True)
     update_e(0, 0, 0)
+    update_e(1, 0, 0)
     settle(gather)
-    inject(0)
-    update_e(1, 0, 0)
+    inject_late()
     inject(1)
+    update_h(0, 1, False)
+    update_e(0, 1, 1)
+    update_h(1, 1, False, True)
+    update_e(1, 1, 1, True)
+    inject(2)
 
     def body(k, carry):
         slot = lax.rem(k, 2)
@@ -500,7 +566,7 @@
 
         return carry
 
-    lax.fori_loop(1, STEPS, body, 0)
+    lax.fori_loop(2, STEPS, body, 0)
 
     squares = jnp.zeros((ny, nz), F32)
     for p in range(nx):
@@ -543,6 +609,9 @@
     dma = pltpu.SemaphoreType.DMA
     block = (nx, ny, nz)
 
+    extended = -(-(nx * ny + 2 * ny + 3 * nx) // 16) * 16
+    flat = -(-(ny + nx) // 16) * 16
+
     def room(*shape):
         return pltpu.VMEM(shape, F32)
 
@@ -564,7 +633,10 @@
             room(STEPS, 3, *block),
             room(STEPS, 3, *block),
             room(STEPS, nx * ny, nz),
-            pltpu.VMEM((nx * ny, count), jnp.bfloat16),
+            room(extended, nz),
+            room(flat, nz),
+            pltpu.VMEM((extended, count), jnp.bfloat16),
+            pltpu.VMEM((flat, count), jnp.bfloat16),
             room(devices, 1, nz),
             room(*block),
             room(2, 2, nx, nz),

time: 35.9 us -> 33.7 us (0.939)
  Pallas kernels: 31.4 us -> 29.3 us
    pallas_call x1, Pallas kernels: 31.4 us -> 29.3 us  [per_device(): pl.pallas_call(functools.partial(kernel, sizes), out_shape=(pltpu.VMEM(bl...]
where the time goes in v3:
time: 33.7 us; the launch traced here: 33.5 us
  Pallas kernels  29.3 us (87%)
  between operations  3.62 us (11%)
  local copies, waits for them, and re-layouts  0.66 us (2%)
    pallas_call x1, Pallas kernels, per_device(): pl.pallas_call(functools.partial(kernel, sizes), out_shape=(pltpu.VMEM(bl...  29.3 us

profile of v3, /device:TPU:0, one launch (start us, length us, event | category | flops | bytes accessed | tf_op | source)
XLA Modules:
  0.0 33.5 jit_solution(4779928980178441085)
XLA Ops:
  1.9 29.3 %shard_map.122 = (f32[8,32,128]{2,1,0:T(8,128)S(1)}, f32[1,1]{1,0:T(1,128)}) custom-call(f32[64]{0:T(128)} %wav_hbm.1, s32[1]{0:T(128)S(6)} %copy.16.src_hbm, s32[1]{0:T(128)S(6)} %copy.17.start_hbm, s32[1,256]{1,0:T(1,128)} %bitcast.2, f32[8,32,128]{2,1,0:T(8,128)} %perm_hbm.1, f32[8,32,128]{2,1,0:T(8,128)} %loss_hbm.1, f32[3,8,32,128]{3,2,1,0:T(8,128)} %fe_hbm.1, ...), custom_call_target="tpu_custom_call" | custom-call | tf_op jit(solution)/shard_map/pallas_call | solution.py:618
  31.2 0.7 %copy.15 = f32[8,32,128]{2,1,0:T(8,128)} copy(f32[8,32,128]{2,1,0:T(8,128)S(1)} %get-tuple-element.6) | data formatting | bytes 262144

commit v4 on v3

--- a/solution.py
+++ b/solution.py
@@ -82,6 +82,7 @@
     g_recv,
     l_send,
     l_recv,
+    told,
     r_send,
     r_recv,
 ):
@@ -112,8 +113,8 @@
     ]
     for load in small:
         load.start()
-    for load in loads:
-        load.start()
+    for i in (0, 2, 1, 3, 4, 5):
+        loads[i].start()
 
     zero_plane = jnp.zeros((ny, nz), F32)
     zero_row = jnp.zeros((1, nz), F32)
@@ -153,8 +154,9 @@
         q = lax.rem(iy + d, gy)
         line.append((q, (ix, q, iz)))
     barrier = pltpu.get_barrier_semaphore()
-    greeted = len(layer) + len(line)
-    for steps in (("+x", "-y"), ("-x", "+y"), ("+y", "-z"), ("-y", "+z")):
+    greeted = len(layer)
+    beside = has["+y"].astype(jnp.int32) + has["-y"].astype(jnp.int32)
+    for steps in (("+y",), ("-y",), ("+x", "-y"), ("-x", "+y"), ("+y", "-z"), ("-y", "+z")):
         dev, can_send, _ = route(steps)
         greeted = greeted + can_send.astype(jnp.int32)
 
@@ -162,7 +164,7 @@
         def _():
             pl.semaphore_signal(barrier, inc=1, device_id=dev, device_id_type=MESH)
 
-    for _, dev in layer + line:
+    for _, dev in layer:
         pl.semaphore_signal(barrier, inc=1, device_id=dev, device_id_type=MESH)
 
     lane = lax.broadcasted_iota(jnp.int32, (ny, nz), 1)
@@ -185,6 +187,18 @@
     for load in small[2:]:
         load.wait()
     pl.semaphore_wait(barrier, greeted)
+
+    def tell(step):
+        for way in ("+y", "-y"):
+            dev, can_send, _ = route((way,))
+
+            @pl.when(can_send)
+            def _():
+                pl.semaphore_signal(told.at[step], inc=1, device_id=dev, device_id_type=MESH)
+
+    hops = gy - 2
+    if hops > 0:
+        tell(0)
 
     def remote(src, dst, ssem, rsem, dev):
         return pltpu.make_async_remote_copy(
@@ -525,7 +539,6 @@
     for s in range(2):
         loads[s].wait()
         send_first(s)
-    for s in range(2):
         loads[2 + s].wait()
         send_magnetic(s)
     loads[4].wait()
@@ -534,6 +547,10 @@
         lo = loss[p]
         keep[p] = (1.0 - lo) / (1.0 + lo)
         curl[p] = 0.5 / (perm[p] * (1.0 + lo))
+    for step in range(hops):
+        pl.semaphore_wait(told.at[step], beside)
+        if step < hops - 1:
+            tell(step + 1)
     settle(gather)
     block = R_all.at[pl.ds(iy * nplane, nplane)]
     gather = exchange(line, iy, block, lambda q: R_all.at[pl.ds(q * nplane, nplane)], l_send, l_recv)
@@ -585,7 +602,9 @@
         q = lax.rem(me + d, devices)
         peers.append((q, (lax.rem(q // gz, gx), q // nplane, lax.rem(q, gz))))
     sums[pl.ds(me, 1)] = part[...]
-    settle(exchange(peers, me, part.at[0], lambda q: sums.at[q], r_send, r_recv))
+    final = exchange(peers, me, part.at[0], lambda q: sums.at[q], r_send, r_recv)
+    for _, recv in final:
+        recv.wait_recv()
     tile = sums[:, 0, :]
     total = jnp.sum(jnp.sum(tile, axis=0, keepdims=True), axis=1, keepdims=True)
     rms = jnp.sqrt(total / (nx * ny * nz * gx * gy * gz) + 1e-06)
@@ -593,6 +612,8 @@
     inverse = 1.0 / rms
     for p in range(nx):
         out_ref[p] = grad[p] * inverse
+    for send, _ in final:
+        send.wait_send()
 
 
 def per_device(
@@ -678,6 +699,7 @@
             dma((gx * gz,)),
             dma((gy,)),
             dma((gy,)),
+            pltpu.SemaphoreType.REGULAR((max(gy - 2, 1),)),
             dma((devices,)),
             dma((devices,)),
         ],

time: 33.7 us -> 33.6 us (level)
  no operation moved by 1% of the time
where the time goes in v4:
time: 33.6 us; the launch traced here: 33.4 us
  Pallas kernels  29.1 us (87%)
  between operations  3.62 us (11%)
  local copies, waits for them, and re-layouts  0.66 us (2%)
    pallas_call x1, Pallas kernels, per_device(): pl.pallas_call(functools.partial(kernel, sizes), out_shape=(pltpu.VMEM(bl...  29.1 us

profile of v4, /device:TPU:0, one launch (start us, length us, event | category | flops | bytes accessed | tf_op | source)
XLA Modules:
  0.0 33.4 jit_solution(3091077917882580753)
XLA Ops:
  1.9 29.1 %shard_map.122 = (f32[8,32,128]{2,1,0:T(8,128)S(1)}, f32[1,1]{1,0:T(1,128)}) custom-call(f32[64]{0:T(128)} %wav_hbm.1, s32[1]{0:T(128)S(6)} %copy.16.src_hbm, s32[1]{0:T(128)S(6)} %copy.17.start_hbm, s32[1,256]{1,0:T(1,128)} %bitcast.2, f32[8,32,128]{2,1,0:T(8,128)} %perm_hbm.1, f32[8,32,128]{2,1,0:T(8,128)} %loss_hbm.1, f32[3,8,32,128]{3,2,1,0:T(8,128)} %fe_hbm.1, ...), custom_call_target="tpu_custom_call" | custom-call | tf_op jit(solution)/shard_map/pallas_call | solution.py:639
  31.0 0.7 %copy.15 = f32[8,32,128]{2,1,0:T(8,128)} copy(f32[8,32,128]{2,1,0:T(8,128)S(1)} %get-tuple-element.6) | data formatting | bytes 262144

commit v5 on v4

--- a/solution.py
+++ b/solution.py
@@ -562,11 +562,11 @@
         update_h(s, 0, True)
     update_e(0, 0, 0)
     update_e(1, 0, 0)
+    update_h(0, 1, False)
+    update_e(0, 1, 1)
     settle(gather)
     inject_late()
     inject(1)
-    update_h(0, 1, False)
-    update_e(0, 1, 1)
     update_h(1, 1, False, True)
     update_e(1, 1, 1, True)
     inject(2)

time: 33.6 us -> 34.5 us (1.027)
  Pallas kernels: 29.1 us -> 30 us
    pallas_call x1, Pallas kernels: 29.1 us -> 30 us  [per_device(): pl.pallas_call(functools.partial(kernel, sizes), out_shape=(pltpu.VMEM(bl...]
where the time goes in v5:
time: 34.5 us; the launch traced here: 34.3 us
  Pallas kernels  30 us (87%)
  between operations  3.62 us (10%)
  local copies, waits for them, and re-layouts  0.66 us (2%)
    pallas_call x1, Pallas kernels, per_device(): pl.pallas_call(functools.partial(kernel, sizes), out_shape=(pltpu.VMEM(bl...  30 us

profile of v5, /device:TPU:0, one launch (start us, length us, event | category | flops | bytes accessed | tf_op | source)
XLA Modules:
  0.0 34.3 jit_solution(17847803454999402381)
XLA Ops:
  1.9 30.0 %shard_map.122 = (f32[8,32,128]{2,1,0:T(8,128)S(1)}, f32[1,1]{1,0:T(1,128)}) custom-call(f32[64]{0:T(128)} %wav_hbm.1, s32[1]{0:T(128)S(6)} %copy.16.src_hbm, s32[1]{0:T(128)S(6)} %copy.17.start_hbm, s32[1,256]{1,0:T(1,128)} %bitcast.2, f32[8,32,128]{2,1,0:T(8,128)} %perm_hbm.1, f32[8,32,128]{2,1,0:T(8,128)} %loss_hbm.1, f32[3,8,32,128]{3,2,1,0:T(8,128)} %fe_hbm.1, ...), custom_call_target="tpu_custom_call" | custom-call | tf_op jit(solution)/shard_map/pallas_call | solution.py:639
  32.0 0.7 %copy.15 = f32[8,32,128]{2,1,0:T(8,128)} copy(f32[8,32,128]{2,1,0:T(8,128)S(1)} %get-tuple-element.6) | data formatting | bytes 262144
